TPU v7x, 32 devices: a whole 2x2x4 slice. The times are simulated.
32 devices in a mesh: rep: 4 (over y, x), shard: 8 (over z, core).
Axes of the slice: x: 2, y: 2, z: 4, core: 2. Of those that a mesh axis runs over, the one named last changes fastest.
Arguments:
- tokens: bfloat16 [16384, 768], P(('rep', 'shard')), may hold values from -6 to 6
- joined_weight: bfloat16 [768, 2304], P('shard'), may hold values from -0.21875 to 0.21875
- mixing_weight: bfloat16 [768, 768], P('shard'), may hold values from -1.25 to 1.25
- gate_weight: bfloat16 [768, 3072], P('shard'), may hold values from -0.21875 to 0.21875
- up_weight: bfloat16 [768, 3072], P('shard'), may hold values from -0.21875 to 0.21875
- down_weight: bfloat16 [3072, 768], P('shard'), may hold values from -0.15625 to 0.15625
- inner_gain: bfloat16 [768], P('shard'), may hold values from 0.5 to 1.5
- inner_shift: bfloat16 [768], P('shard'), may hold values from -1.5 to 1.5
- outer_gain: bfloat16 [768], P('shard'), may hold values from 0.5 to 1.5
- outer_shift: bfloat16 [768], P('shard'), may hold values from -1.5 to 1.5
- segments: int32 [32, 512], P(('rep', 'shard')), may hold values from 0 to 3, as said below
- positions: int32 [32, 512], P(('rep', 'shard')), may hold values from 0 to 255, as said below
- cotangent: bfloat16 [16384, 768], P(('rep', 'shard')), may hold values from -6 to 6
Outputs:
- layer_output: bfloat16 [16384, 768], P(('rep', 'shard'))
- input_grad: bfloat16 [16384, 768], P(('rep', 'shard'))
- joined_grad: float32 [768, 2304], P('shard')
- mixing_grad: float32 [768, 768], P('shard')
- gate_grad: float32 [768, 3072], P('shard')
- up_grad: float32 [768, 3072], P('shard')
- down_grad: float32 [3072, 768], P('shard')
- innergain_grad: float32 [768], P('shard')
- innershift_grad: float32 [768], P('shard')
- outergain_grad: float32 [768], P('shard')
- outershift_grad: float32 [768], P('shard')
Inputs may be any that keep to these rules, and one draw needn't show every extreme that they name: `segments`: each sequence of 512 tokens packs 4 documents in order: segment numbers never fall along a sequence and each appears; each document holds 32 to 256 tokens, and exactly one holds 256. `positions`: A token's position counts the tokens before it in its own document.
All inputs are finite; a program needn't handle non-finite values.
Results may differ from a plain program's by a relative error of at most 0.02.
Values may be sent and summed in bfloat16 or wider, within the bound.
A program may use at most 128 MiB of HBM per device.

v0:
```python
import math

import jax
import jax.numpy as jnp
from jax import lax
from jax.sharding import PartitionSpec as P

H = 12
HD = 64


EPSILON = 1e-12
NEG_LARGE = -1e30


def rotation(positions):
    halves = jnp.arange(HD // 2, dtype=jnp.float32)
    inverse = 1000.0 ** (-(2.0 * halves) / HD)
    angles = positions.astype(jnp.float32)[..., None] * inverse
    angles = jnp.concatenate([angles, angles], axis=-1)
    return (jnp.cos(angles), jnp.sin(angles))


def rotate(values, cosine, sine_table):
    half_size = values.shape[-1] // 2
    turned = jnp.concatenate([-values[..., half_size:], values[..., :half_size]], axis=-1)
    return values * cosine[..., None, :] + turned * sine_table[..., None, :]


def layer_norm(values, gain, shift):
    centred = values - jnp.mean(values, axis=-1, keepdims=True)
    variance = jnp.mean(centred * centred, axis=-1, keepdims=True)
    return centred * lax.rsqrt(variance + EPSILON) * gain + shift


def transposed_product(left, right):
    return lax.dot_general(
        left, right, (((1,), (1,)), ((), ())), preferred_element_type=jnp.float32
    )


def token_contract(left, right):
    return lax.dot_general(
        left, right, (((0,), (0,)), ((), ())), preferred_element_type=jnp.float32
    )


def to_heads(values, group_size):
    length = values.shape[0]
    per_head = values.reshape(length, H, HD).transpose(1, 0, 2)
    return per_head.reshape(H // group_size, group_size, length, HD)


def from_heads(values):
    length = values.shape[2]
    merged = values.reshape(H, length, HD).transpose(1, 0, 2)
    return merged.reshape(length, H * HD)


def on_device(
    tokens,
    joined_weight,
    mixing_weight,
    gate_weight,
    up_weight,
    down_weight,
    inner_gain,
    inner_shift,
    outer_gain,
    outer_shift,
    segments,
    positions,
    cotangent,
):
    joined_full, mixing_full, innergain_full, innershift_full = (
        lax.all_gather(joined_weight, "shard", axis=0, tiled=True),
        lax.all_gather(mixing_weight, "shard", axis=0, tiled=True),
        lax.all_gather(inner_gain, "shard", axis=0, tiled=True),
        lax.all_gather(inner_shift, "shard", axis=0, tiled=True),
    )
    gate_full, upward_full, down_full, outergain_full, outershift_full = (
        lax.all_gather(gate_weight, "shard", axis=0, tiled=True),
        lax.all_gather(up_weight, "shard", axis=0, tiled=True),
        lax.all_gather(down_weight, "shard", axis=0, tiled=True),
        lax.all_gather(outer_gain, "shard", axis=0, tiled=True),
        lax.all_gather(outer_shift, "shard", axis=0, tiled=True),
    )
    length = tokens.shape[0]
    model_width = tokens.shape[1]
    group_size = 4
    score_scale = 1.0 / math.sqrt(HD)
    same_doc = segments[0][:, None] == segments[0][None, :]
    cosine, sine_table = rotation(positions[0])
    joined_rows = jnp.dot(tokens, joined_full, preferred_element_type=jnp.float32)
    pre_query = joined_rows[:, :model_width].reshape(length, H, HD)
    pre_key = joined_rows[:, model_width : 2 * model_width].reshape(length, H, HD)
    rotated_pair, rotate_pull = jax.vjp(
        lambda first, second: (
            rotate(first, cosine, sine_table),
            rotate(second, cosine, sine_table),
        ),
        pre_query,
        pre_key,
    )
    query_heads = to_heads(
        rotated_pair[0].astype(jnp.bfloat16).reshape(length, model_width), group_size
    )
    key_heads = to_heads(
        rotated_pair[1].astype(jnp.bfloat16).reshape(length, model_width), group_size
    )
    value_heads = to_heads(joined_rows[:, 2 * model_width :].astype(jnp.bfloat16), group_size)

    def head_scores(query_block, key_block):
        scores = (
            jnp.einsum("hqd,hkd->hqk", query_block, key_block, preferred_element_type=jnp.float32)
            * score_scale
        )
        return jnp.where(same_doc, scores, NEG_LARGE)

    def head_forward(block):
        query_block, key_block, value_block = block
        scores = head_scores(query_block, key_block)
        highest = jnp.max(scores, axis=-1, keepdims=True)
        shifted = jnp.exp(scores - highest)
        denominator = jnp.sum(shifted, axis=-1, keepdims=True)
        probs_low = (shifted / denominator).astype(jnp.bfloat16)
        attended = jnp.einsum(
            "hqk,hkd->hqd", probs_low, value_block, preferred_element_type=jnp.float32
        )
        return (attended.astype(jnp.bfloat16), highest + jnp.log(denominator))

    attended_heads, logsum = lax.map(head_forward, (query_heads, key_heads, value_heads))
    attended_low = from_heads(attended_heads)
    branch = jnp.dot(attended_low, mixing_full, preferred_element_type=jnp.float32)
    inner_resid = tokens.astype(jnp.float32) + branch
    normed, inner_pull = jax.vjp(
        layer_norm,
        inner_resid,
        innergain_full.astype(jnp.float32),
        innershift_full.astype(jnp.float32),
    )
    normed_low = normed.astype(jnp.bfloat16)
    gate_rows = jnp.dot(normed_low, gate_full, preferred_element_type=jnp.float32)
    upward = jnp.dot(normed_low, upward_full, preferred_element_type=jnp.float32)
    active, silu_pull = jax.vjp(
        lambda first, second: jax.nn.silu(first) * second, gate_rows, upward
    )
    active_low = active.astype(jnp.bfloat16)
    result = jnp.dot(active_low, down_full, preferred_element_type=jnp.float32)
    final, outer_pull = jax.vjp(
        layer_norm,
        normed + result,
        outergain_full.astype(jnp.float32),
        outershift_full.astype(jnp.float32),
    )
    layer_output = final.astype(jnp.bfloat16)
    gate_back, upward_back, down_back = (
        lax.all_gather(gate_weight, "shard", axis=0, tiled=True),
        lax.all_gather(up_weight, "shard", axis=0, tiled=True),
        lax.all_gather(down_weight, "shard", axis=0, tiled=True),
    )
    outer_grad, outergain_grad, outershift_grad = outer_pull(cotangent.astype(jnp.float32))
    result_grad = outer_grad.astype(jnp.bfloat16)
    down_grad = token_contract(active_low, result_grad)
    active_grad = transposed_product(result_grad, down_back)
    gate_part, upward_part = silu_pull(active_grad)
    gate_low = gate_part.astype(jnp.bfloat16)
    upward_low = upward_part.astype(jnp.bfloat16)
    gate_grad = token_contract(normed_low, gate_low)
    up_grad = token_contract(normed_low, upward_low)
    normed_grad = (
        outer_grad
        + transposed_product(gate_low, gate_back)
        + transposed_product(upward_low, upward_back)
    )
    inner_grad, innergain_grad, innershift_grad = inner_pull(normed_grad)
    dense_sums = (
        lax.psum_scatter(
            gate_grad.astype(jnp.bfloat16), "shard", scatter_dimension=0, tiled=True
        ).astype(jnp.float32),
        lax.psum_scatter(
            up_grad.astype(jnp.bfloat16), "shard", scatter_dimension=0, tiled=True
        ).astype(jnp.float32),
        lax.psum_scatter(
            down_grad.astype(jnp.bfloat16), "shard", scatter_dimension=0, tiled=True
        ).astype(jnp.float32),
        lax.psum_scatter(
            outergain_grad.astype(jnp.bfloat16), "shard", scatter_dimension=0, tiled=True
        ).astype(jnp.float32),
        lax.psum_scatter(
            outershift_grad.astype(jnp.bfloat16), "shard", scatter_dimension=0, tiled=True
        ).astype(jnp.float32),
        lax.psum_scatter(
            innergain_grad.astype(jnp.bfloat16), "shard", scatter_dimension=0, tiled=True
        ).astype(jnp.float32),
        lax.psum_scatter(
            innershift_grad.astype(jnp.bfloat16), "shard", scatter_dimension=0, tiled=True
        ).astype(jnp.float32),
    )
    joined_back, mixing_back = (
        lax.all_gather(joined_weight, "shard", axis=0, tiled=True),
        lax.all_gather(mixing_weight, "shard", axis=0, tiled=True),
    )
    branch_grad = inner_grad.astype(jnp.bfloat16)
    mixing_grad = token_contract(attended_low, branch_grad)
    attended_grad = transposed_product(branch_grad, mixing_back).astype(jnp.bfloat16)

    def head_backward(block):
        query_block, key_block, value_block, output_block, logsum_block = block
        probability = jnp.exp(head_scores(query_block, key_block) - logsum_block)
        prob_grad = jnp.einsum(
            "hqd,hkd->hqk", output_block, value_block, preferred_element_type=jnp.float32
        )
        value_grad = jnp.einsum(
            "hqk,hqd->hkd",
            probability.astype(jnp.bfloat16),
            output_block,
            preferred_element_type=jnp.float32,
        )
        row_dot = jnp.sum(probability * prob_grad, axis=-1, keepdims=True)
        score_grad = (probability * (prob_grad - row_dot)).astype(jnp.bfloat16)
        query_grad = (
            jnp.einsum("hqk,hkd->hqd", score_grad, key_block, preferred_element_type=jnp.float32)
            * score_scale
        )
        key_grad = (
            jnp.einsum("hqk,hqd->hkd", score_grad, query_block, preferred_element_type=jnp.float32)
            * score_scale
        )
        return (query_grad, key_grad, value_grad)

    query_grad, key_grad, value_grad = lax.map(
        head_backward,
        (query_heads, key_heads, value_heads, to_heads(attended_grad, group_size), logsum),
    )
    query_raw, key_raw = rotate_pull(
        (from_heads(query_grad).reshape(length, H, HD), from_heads(key_grad).reshape(length, H, HD))
    )
    joined_low = jnp.concatenate(
        [
            query_raw.reshape(length, model_width),
            key_raw.reshape(length, model_width),
            from_heads(value_grad),
        ],
        axis=1,
    ).astype(jnp.bfloat16)
    input_grad = (inner_grad + transposed_product(joined_low, joined_back)).astype(jnp.bfloat16)
    joined_grad = token_contract(tokens, joined_low)
    mixer_sums = (
        lax.psum_scatter(
            joined_grad.astype(jnp.bfloat16), "shard", scatter_dimension=0, tiled=True
        ).astype(jnp.float32),
        lax.psum_scatter(
            mixing_grad.astype(jnp.bfloat16), "shard", scatter_dimension=0, tiled=True
        ).astype(jnp.float32),
    )
    summed = (
        lax.psum(mixer_sums[0].astype(jnp.bfloat16), "rep").astype(jnp.float32),
        lax.psum(mixer_sums[1].astype(jnp.bfloat16), "rep").astype(jnp.float32),
        lax.psum(dense_sums[0].astype(jnp.bfloat16), "rep").astype(jnp.float32),
        lax.psum(dense_sums[1].astype(jnp.bfloat16), "rep").astype(jnp.float32),
        lax.psum(dense_sums[2].astype(jnp.bfloat16), "rep").astype(jnp.float32),
        lax.psum(dense_sums[3].astype(jnp.bfloat16), "rep").astype(jnp.float32),
        lax.psum(dense_sums[4].astype(jnp.bfloat16), "rep").astype(jnp.float32),
        lax.psum(dense_sums[5].astype(jnp.bfloat16), "rep").astype(jnp.float32),
        lax.psum(dense_sums[6].astype(jnp.bfloat16), "rep").astype(jnp.float32),
    )
    return (
        layer_output,
        input_grad,
        summed[0],
        summed[1],
        summed[2],
        summed[3],
        summed[4],
        summed[7],
        summed[8],
        summed[5],
        summed[6],
    )


def solution(mesh):
    placed = (
        P(("rep", "shard"), None),
        P("shard", None),
        P("shard", None),
        P("shard", None),
        P("shard", None),
        P("shard", None),
        P("shard"),
        P("shard"),
        P("shard"),
        P("shard"),
        P(("rep", "shard"), None),
        P(("rep", "shard"), None),
        P(("rep", "shard"), None),
    )
    return jax.shard_map(
        on_device,
        mesh=mesh,
        in_specs=placed,
        out_specs=(
            P(("rep", "shard"), None),
            P(("rep", "shard"), None),
            P("shard", None),
            P("shard", None),
            P("shard", None),
            P("shard", None),
            P("shard", None),
            P("shard"),
            P("shard"),
            P("shard"),
            P("shard"),
        ),
        check_vma=False,
    )
```

profile of v0, /device:TPU:0, one launch (start us, length us, event | category | flops | bytes accessed | tf_op | source)
XLA Modules:
  0.0 650.4 jit_solution(14703925694465118781)
XLA Ops:
  13.1 19.2 %all-reduce.13 = (bf16[768]{0:T(1024)(128)(2,1)S(1)}, bf16[768]{0:T(1024)(128)(2,1)S(1)}, bf16[768]{0:T(1024)(128)(2,1)S(1)}) all-reduce(bf16[768]{0:T(1024)(128)(2,1)S(1)} %dynamic-update-slice.1, bf16[768]{0:T(1024)(128)(2,1)S(1)} %dynamic-update-slice, ...), channel_id=1, replica_groups=mesh['rep'=4,'shard'=8] {'shard'}, use_global_device_ids=true, to_apply=%add.5 | all-reduce | flops 2304 | bytes 9216
  32.4 21.9 %all-gather.6.cloned.1.call-done = bf16[768,2304]{1,0:T(8,128)(2,1)} async-done(((bf16[96,2304]{1,0:T(8,128)(2,1)}), bf16[768,2304]{1,0:T(8,128)(2,1)}) %all-gather.6.cloned.1.call-update) | async-done | bytes 3538960 | tf_op jit(solution)/shard_map/all_gather | solution.py:76
  54.3 4.0 fusion.91
  58.3 1.3 fusion.85
  61.0 1.9 copy.49
  63.0 2.9 copy.50
  66.3 2.3 fusion.70
  68.6 15.4 %while.28 = (s32[]{:T(128)}, bf16[3,4,512,64]{2,3,1,0:T(8,128)(2,1)}, f32[3,4,512,1]{2,1,3,0:T(4,128)S(1)}, bf16[3,4,512,64]{2,3,1,0:T(8,128)(2,1)S(1)}, bf16[3,...) while((s32[]{:T(128)}, ...), condition=%wide.region_3.4_spmd.clone, body=%wide.region_0.3_spmd.clone.sunk | while | flops 281409536 | bytes 14749785 | solution.py:132
  70.7 3.0 fusion.139
  75.8 3.1 fusion.139
  81.0 3.0 fusion.139
  84.0 2.7 fusion.89
  87.1 1.2 fusion.75
  88.3 41.8 %all-gather.10.cloned.1.call-done = bf16[768,3072]{1,0:T(8,128)(2,1)} async-done(((bf16[96,3072]{1,0:T(8,128)(2,1)}), bf16[768,3072]{1,0:T(8,128)(2,1)}) %all-gather.10.cloned.1.call-update) | async-done | bytes 4718608 | tf_op jit(solution)/shard_map/all_gather | solution.py:82
  130.1 7.9 %fusion.92 = f32[512,3072]{1,0:T(8,128)} fusion(bf16[512,768]{1,0:T(8,128)(2,1)} %fusion.75, bf16[768,3072]{1,0:T(8,128)(2,1)} %all-gather.10.cloned.1.call-done), kind=kOutput, calls=%fused_computation.148 | convolution fusion | flops 2415919104 | bytes 11796480 | tf_op jit(solution)/shard_map/dot_general | solution.py:143
  138.0 43.6 %all-gather.12.cloned.1.call-done = bf16[768,3072]{1,0:T(8,128)(2,1)} async-done(((bf16[96,3072]{1,0:T(8,128)(2,1)}), bf16[768,3072]{1,0:T(8,128)(2,1)}) %all-gather.12.cloned.1.call-update) | async-done | bytes 4718608 | tf_op jit(solution)/shard_map/all_gather | solution.py:83
  181.6 9.1 %multiply_convert_fusion.2 = (bf16[512,3072]{1,0:T(8,128)(2,1)}, f32[512,3072]{1,0:T(8,128)}) fusion(f32[512,3072]{1,0:T(8,128)} %fusion.92, bf16[512,768]{1,0:T(8,128)(2,1)S(1)} %copy-done.9, bf16[768,3072]{1,0:T(8,128)(2,1)} %all-gather.12.cloned.1.call-done), kind=kOutput, calls=%fused_computation.68 | convolution fusion | flops 2425356288 | bytes 21233664 | tf_op jit(solution)/shard_map/dot_general | solution.py:144
  190.7 42.4 %all-gather.14.cloned.1.call-done = bf16[3072,768]{1,0:T(8,128)(2,1)} async-done(((bf16[384,768]{1,0:T(8,128)(2,1)}), bf16[3072,768]{1,0:T(8,128)(2,1)}) %all-gather.14.cloned.1.call-update) | async-done | bytes 4718608 | tf_op jit(solution)/shard_map/all_gather | solution.py:84
  233.1 6.4 fusion.90
  242.1 1.9 copy-done.5
  244.0 10.3 %multiply_convert_fusion.1 = (bf16[512,3072]{1,0:T(8,128)(2,1)}, bf16[512,3072]{1,0:T(8,128)(2,1)}) fusion(f32[512,3072]{1,0:T(8,128)S(1)} %copy-done.5, f32[512,3072]{1,0:T(8,128)} %get-tuple-element.270, bf16[3072,768]{1,0:T(8,128)(2,1)} %all-gather.14.cloned.1.call-done, f32[512,768]{1,0:T(8,128)S(1)} %get-tuple-element.240, ...), kind=kOutput, calls=%fused_computation.67 | convolution fusion | flops 2438725632 | bytes 25167872 | tf_op jit(solution)/shard_map/dot_general | solution.py:37
  254.4 4.7 fusion.93
  259.2 3.2 multiply_reduce_fusion.1
  263.1 1.2 copy-done.13
  264.3 1.7 convolution_convert_fusion.5
  266.0 2.3 copy.51
  268.3 29.1 %while.29 = (s32[]{:T(128)}, f32[3,4,512,64]{2,3,1,0:T(8,128)}, f32[3,4,512,64]{2,3,1,0:T(8,128)}, bf16[3,4,512,64]{2,3,1,0:T(8,128)(2,1)}, bf16[3,4,512,64]{2,3...) while((s32[]{:T(128)}, f32[3,4,512,64]{2,3,1,0:T(8,128)}, ...), condition=%wide.region_14.15_spmd.clone, body=%wide.region_12.14_spmd.clone.sunk | while | flops 687339520 | bytes 39124108 | solution.py:232
  269.5 2.5 multiply_reduce_fusion.6
  271.9 1.2 multiply_convert_fusion.4
  273.2 1.6 fusion.150
  274.7 1.3 fusion.149
  276.0 2.0 fusion.151
  279.1 2.5 multiply_reduce_fusion.6
  281.6 1.2 multiply_convert_fusion.4
  282.8 1.5 fusion.150
  284.4 1.3 fusion.149
  285.6 2.0 fusion.151
  288.7 2.5 multiply_reduce_fusion.6
  291.2 1.2 multiply_convert_fusion.4
  292.4 1.6 fusion.150
  294.0 1.3 fusion.149
  295.3 2.0 fusion.151
  297.4 2.3 bitcast_multiply_fusion.2
  300.0 1.2 copy-done.6
  303.8 4.9 fusion.62
  308.7 5.8 copy.57
  314.6 3.7 convolution_convert_fusion.4
  318.3 7.1 %convolution_convert_fusion = bf16[3072,768]{1,0:T(8,128)(2,1)} fusion(bf16[512,3072]{1,0:T(8,128)(2,1)} %get-tuple-element.269, f32[512,768]{1,0:T(8,128)S(1)} %copy-done.12, f32[512]{0:T(512)S(1)} %negate_multiply_fusion.1), kind=kOutput, calls=%fused_computation.71 | convolution fusion | flops 2419064832 | bytes 9439232 | tf_op jit(solution)/shard_map/dot_general | solution.py:43
  326.5 6.2 convolution_convert_fusion.2
  332.8 6.3 convolution_convert_fusion.1
  339.2 18.0 %reduce-scatter.16.cloned.1.call-done = bf16[96,2304]{1,0:T(8,128)(2,1)} async-done(((bf16[768,2304]{1,0:T(8,128)(2,1)}), bf16[96,2304]{1,0:T(8,128)(2,1)}) %reduce-scatter.16.cloned.1.call-update) | async-done | bytes 442384
  357.1 2.1 copy.58
  359.2 32.3 %reduce-scatter.8.cloned.1.call-done = bf16[96,768]{1,0:T(8,128)(2,1)} async-done(((bf16[768,768]{1,0:T(8,128)(2,1)}), bf16[96,768]{1,0:T(8,128)(2,1)}) %reduce-scatter.8.cloned.1.call-update) | async-done | bytes 147472 | tf_op jit(solution)/shard_map/reduce_scatter | solution.py:253
  391.5 55.4 %reduce-scatter.14.cloned.1.call-done = bf16[384,768]{1,0:T(8,128)(2,1)} async-done(((bf16[3072,768]{1,0:T(8,128)(2,1)}), bf16[384,768]{1,0:T(8,128)(2,1)}) %reduce-scatter.14.cloned.1.call-update) | async-done | bytes 589840 | tf_op jit(solution)/shard_map/reduce_scatter | solution.py:184
  446.9 55.7 %reduce-scatter.10.cloned.1.call-done = bf16[96,3072]{1,0:T(8,128)(2,1)} async-done(((bf16[768,3072]{1,0:T(8,128)(2,1)}), bf16[96,3072]{1,0:T(8,128)(2,1)}) %reduce-scatter.10.cloned.1.call-update) | async-done | bytes 589840 | tf_op jit(solution)/shard_map/reduce_scatter | solution.py:178
  502.6 55.5 %reduce-scatter.12.cloned.1.call-done = bf16[96,3072]{1,0:T(8,128)(2,1)} async-done(((bf16[768,3072]{1,0:T(8,128)(2,1)}), bf16[96,3072]{1,0:T(8,128)(2,1)}) %reduce-scatter.12.cloned.1.call-update) | async-done | bytes 589840 | tf_op jit(solution)/shard_map/reduce_scatter | solution.py:181
  559.6 25.9 %all-reduce.12 = (bf16[768]{0:T(1024)(128)(2,1)S(1)}, bf16[768]{0:T(1024)(128)(2,1)S(1)}, bf16[768]{0:T(1024)(128)(2,1)S(1)}, bf16[768]{0:T(1024)(128)(2,1)S(1)}, bf16[768]{0:T(1024)(128)(2,1)S(1)}) all-reduce(bf16[768]{0:T(1024)(128)(2,1)S(1)} %dynamic-update-slice.3, ...), channel_id=1, replica_groups=mesh['rep'=4,'shard'=8] {'shard'}, use_global_device_ids=true, to_apply=%add.7 | all-reduce | flops 3840 | bytes 15360
  585.8 10.7 %all-reduce.14 = (bf16[96]{0:T(256)(128)(2,1)S(1)}, bf16[96]{0:T(256)(128)(2,1)S(1)}, bf16[96]{0:T(256)(128)(2,1)S(1)}, bf16[96]{0:T(256)(128)(2,1)S(1)}) all-reduce(bf16[96]{0:T(256)(128)(2,1)S(1)} %dynamic-slice.5, bf16[96]{0:T(256)(128)(2,1)S(1)} %dynamic-slice.7, ...), channel_id=1, replica_groups=mesh['rep'=4,'shard'=8] {'rep'}, use_global_device_ids=true, to_apply=%region_27.28 | all-reduce | flops 384 | bytes 1536 | tf_op jit(solution)/shard_map/psum | solution.py:265
  598.6 1.2 add_convert_fusion.1
  599.8 5.4 add_convert_fusion
  605.2 32.0 %all-reduce.18.cloned.1.call-done = (bf16[96,2304]{0,1:T(8,128)(2,1)}, bf16[96,768]{1,0:T(8,128)(2,1)}, bf16[96,3072]{1,0:T(8,128)(2,1)}, bf16[96,3072]{1,0:T(8,128)(2,1)}, bf16[384,768]{1,0:T(8,128)(2,1)}) async-done(((bf16[96,2304]{0,1:T(8,128)(2,1)}, bf16[96,768]{1,0:T(8,128)(2,1)}, bf16[96,3072]{1,0:T(8,128)(2,1)}, bf16[96,3072]{1,0:T(8,128)(2,1)}, bf16[384,768]{1,0:T(8,128)(2,1)}), ...) | async-done | bytes 2359312 | tf_op jit(solution)/shard_map/psum | solution.py:258
  637.2 2.3 convert_element_type.173
  639.5 1.1 convert_element_type.175
  641.7 1.2 copy.52
  (181 shorter events, 29.1 us)
Async XLA Ops:
  7.2 4.0 copy-start.27
  7.2 3.6 copy-start.28
  7.2 5.2 copy-start.32
  7.2 5.4 copy-start.33
  7.2 5.7 copy-start.34
  7.2 47.0 %copy-start.30 = (bf16[512,768]{1,0:T(8,128)(2,1)S(1)}, bf16[512,768]{1,0:T(8,128)(2,1)}, u32[]{:S(2)}) copy-start(bf16[512,768]{1,0:T(8,128)(2,1)} %param.17) | copy-start | bytes 2359300
  7.2 47.0 %all-gather.6.cloned.1.call-start = ((), (), s32[]{:S(2)}) async-start(), calls=%async_computation.5 | async-start | bytes 3981312 | tf_op jit(solution)/shard_map/all_gather | solution.py:76
  8.0 76.0 %all-gather.8.cloned.1.call-start = ((), (), s32[]{:S(2)}) async-start(), calls=%async_computation.6 | async-start | bytes 1327104 | tf_op jit(solution)/shard_map/all_gather | solution.py:77
  8.7 121.4 %all-gather.10.cloned.1.call-start = ((), (), s32[]{:S(2)}) async-start(), calls=%async_computation.7 | async-start | bytes 5308416 | tf_op jit(solution)/shard_map/all_gather | solution.py:82
  9.5 172.1 %all-gather.12.cloned.1.call-start = ((), (), s32[]{:S(2)}) async-start(), calls=%async_computation.8 | async-start | bytes 5308416 | tf_op jit(solution)/shard_map/all_gather | solution.py:83
  10.0 223.0 %all-gather.14.cloned.1.call-start = ((), (), s32[]{:S(2)}) async-start(), calls=%async_computation.9 | async-start | bytes 5308416 | tf_op jit(solution)/shard_map/all_gather | solution.py:84
  10.6 346.5 %reduce-scatter.16.cloned.1.call-start = ((), (), s32[]{:S(2)}) async-start(), calls=%async_computation.14 | async-start | bytes 3981312
  11.1 55.2 %copy-start.15 = (f32[512,64]{0,1:T(8,128)}, f32[512,64]{0,1:T(8,128)S(1)}, u32[]{:S(2)}) copy-start(f32[512,64]{0,1:T(8,128)S(1)} %get-tuple-element.263) | copy-start | bytes 393220
  11.1 55.2 %copy-start.17 = (f32[512,64]{0,1:T(8,128)}, f32[512,64]{0,1:T(8,128)S(1)}, u32[]{:S(2)}) copy-start(f32[512,64]{0,1:T(8,128)S(1)} %get-tuple-element.264) | copy-start | bytes 393220
  63.0 3.3 copy-start.2
  66.3 2.3 copy-start.19
  86.7 1.5 copy-start
  130.1 51.5 %copy-start.9 = (bf16[512,768]{1,0:T(8,128)(2,1)S(1)}, bf16[512,768]{1,0:T(8,128)(2,1)}, u32[]{:S(2)}) copy-start(bf16[512,768]{1,0:T(8,128)(2,1)} %fusion.75) | copy-start | bytes 2359300
  239.5 1.1 copy-start.3
  240.6 3.4 copy-start.5
  241.4 12.9 %slice-start = ((s8[4718592]{0:T(1024)(128)(4,1)}), s8[524288]{0:T(1024)(128)(4,1)S(1)}, s32[]{:S(2)}) async-start(s8[4718592]{0:T(1024)(128)(4,1)} %bitcast.188), calls=%async_computation.16 | async-start | bytes 1048576
  241.4 17.7 %slice-start.2 = ((s8[4718592]{0:T(1024)(128)(4,1)}), s8[4194304]{0:T(1024)(128)(4,1)S(1)}, s32[]{:S(2)}) async-start(s8[4718592]{0:T(1024)(128)(4,1)} %bitcast.196), calls=%async_computation.18 | async-start | bytes 8388608
  242.1 17.0 %copy-start.11 = (f32[512,768]{1,0:T(8,128)}, f32[512,768]{1,0:T(8,128)S(1)}, u32[]{:S(2)}) copy-start(f32[512,768]{1,0:T(8,128)S(1)} %get-tuple-element.240) | copy-start | bytes 4718596
  244.0 10.3 %slice-start.1 = ((s8[4718592]{0:T(1024)(128)(4,1)}), s8[4194304]{0:T(1024)(128)(4,1)S(1)}, s32[]{:S(2)}) async-start(s8[4718592]{0:T(1024)(128)(4,1)} %bitcast.188), calls=%async_computation.17 | async-start | bytes 8388608
  244.0 15.1 %slice-start.3 = ((s8[4718592]{0:T(1024)(128)(4,1)}), s8[524288]{0:T(1024)(128)(4,1)S(1)}, s32[]{:S(2)}) async-start(s8[4718592]{0:T(1024)(128)(4,1)} %bitcast.196), calls=%async_computation.19 | async-start | bytes 1048576
  254.3 4.8 copy-start.1
  254.4 4.8 copy-start.36
  262.4 1.9 copy-start.29
  263.1 1.2 copy-start.13
  268.3 29.1 %copy-start.18 = (f32[512,64]{0,1:T(8,128)S(1)}, f32[512,64]{0,1:T(8,128)}, u32[]{:S(2)}) copy-start(f32[512,64]{0,1:T(8,128)} %copy-done.17) | copy-start | bytes 393220
  268.3 1.2 copy-start.8
  278.0 1.1 copy-start.8
  287.6 1.1 copy-start.8
  297.4 2.6 copy-start.16
  299.9 1.4 copy-start.6
  299.9 1.9 copy-start.7
  301.7 2.0 copy-start.31
  302.6 0.9 copy-start.20
  302.7 1.1 copy-start.22
  314.5 3.8 copy-start.12
  314.5 77.0 %reduce-scatter.8.cloned.1.call-start = ((), (), s32[]{:S(2)}) async-start(), calls=%async_computation.10 | async-start | bytes 1327104 | tf_op jit(solution)/shard_map/reduce_scatter | solution.py:253
  318.2 128.7 %reduce-scatter.14.cloned.1.call-start = ((), (), s32[]{:S(2)}) async-start(), calls=%async_computation.13 | async-start | bytes 5308416 | tf_op jit(solution)/shard_map/reduce_scatter | solution.py:184
  325.4 1.1 copy-start.10
  325.4 177.2 %reduce-scatter.10.cloned.1.call-start = ((), (), s32[]{:S(2)}) async-start(), calls=%async_computation.11 | async-start | bytes 5308416 | tf_op jit(solution)/shard_map/reduce_scatter | solution.py:178
  332.8 225.4 %reduce-scatter.12.cloned.1.call-start = ((), (), s32[]{:S(2)}) async-start(), calls=%async_computation.12 | async-start | bytes 5308416 | tf_op jit(solution)/shard_map/reduce_scatter | solution.py:181
  339.1 219.0 %copy-start.4 = (bf16[512,768]{1,0:T(8,128)(2,1)S(1)}, bf16[512,768]{1,0:T(8,128)(2,1)}, u32[]{:S(2)}) copy-start(bf16[512,768]{1,0:T(8,128)(2,1)} %param.29) | copy-start | bytes 2359300
  339.1 298.1 %all-reduce.18.cloned.1.call-start = ((), (), s32[]{:S(2)}) async-start(), calls=%async_computation.15 | async-start | bytes 5013504 | tf_op jit(solution)/shard_map/psum | solution.py:258
  558.1 0.7 copy-start.35
  558.3 41.4 %copy-start.14 = (f32[512,768]{1,0:T(8,128)S(1)}, f32[512,768]{1,0:T(8,128)}, u32[]{:S(2)}) copy-start(f32[512,768]{1,0:T(8,128)} %copy-done.13) | copy-start | bytes 4718596
  596.5 3.3 copy-start.21
  637.2 2.3 copy-start.24
  637.2 3.4 copy-start.23
  639.5 2.2 copy-start.25
  640.6 2.2 copy-start.26
Sparse Core Ops, SparseCore 0:
  9.7 44.5 all-gather.5
  55.9 21.6 all-gather.7
  79.2 50.8 all-gather.9
  131.6 49.9 all-gather.11
  183.1 49.9 all-gather.13
  314.6 42.4 reduce-scatter.15
  360.0 31.5 reduce-scatter.7
  393.8 53.0 reduce-scatter.13
  449.2 53.3 reduce-scatter.9
  504.7 53.3 reduce-scatter.11
  561.9 75.2 all-reduce.17
where the time goes:
time: 660 us; the launch traced here: 650 us
  waiting for transfers between devices  402 us (61%)
  matrix products  120 us (18%)
  blocking collectives  55.8 us (8%)
  local copies, waits for them, and re-layouts  29.5 us (4%)
  other arithmetic  26.8 us (4%)
  between operations  16.1 us (2%)
    reduce_scatter x1, waiting for transfers between devices, on_device(): lax.psum_scatter(gate_grad.astype(jnp.bfloat16), 'shard', scatter_dimensi...  55.7 us
    reduce_scatter x1, waiting for transfers between devices, on_device(): lax.psum_scatter(up_grad.astype(jnp.bfloat16), 'shard', scatter_dimension...  55.5 us
    reduce_scatter x1, waiting for transfers between devices, on_device(): lax.psum_scatter(down_grad.astype(jnp.bfloat16), 'shard', scatter_dimensi...  55.4 us
    unnamed x2, blocking collectives  45.1 us
    all_gather x1, waiting for transfers between devices, on_device(): lax.all_gather(up_weight, 'shard', axis=0, tiled=True)  43.6 us
    all_gather x1, waiting for transfers between devices, on_device(): lax.all_gather(down_weight, 'shard', axis=0, tiled=True)  42.4 us
    all_gather x1, waiting for transfers between devices, on_device(): lax.all_gather(gate_weight, 'shard', axis=0, tiled=True)  41.8 us
    reduce_scatter x1, waiting for transfers between devices, on_device(): lax.psum_scatter(mixing_grad.astype(jnp.bfloat16), 'shard', scatter_dimen...  32.3 us
  transfers between devices with their start and end apart: 11, of which 10 were waited for; matrix products, arithmetic and copies ran while one was open for 13% of the time, Pallas kernels for 0%

commit v1 on v0

--- a/solution.py
+++ b/solution.py
@@ -1,16 +1,543 @@
+import functools
 import math
 
 import jax
 import jax.numpy as jnp
 from jax import lax
+from jax.experimental import pallas as pl
+from jax.experimental.pallas import tpu as pltpu
 from jax.sharding import PartitionSpec as P
 
 H = 12
 HD = 64
 
-
 EPSILON = 1e-12
 NEG_LARGE = -1e30
+LANES = 128
+MESH = pl.DeviceIdType.MESH
+VMEM_LIMIT = 62 * 1024 * 1024
+
+
+class Plan:
+    def __init__(self, width, replicas, shards):
+        self.replicas, self.shards = replicas, shards
+        self.chips = shards // 2
+        self.levels = replicas.bit_length() - 1
+        self.orders = 2 if self.levels > 1 and width % (2 * replicas * LANES) == 0 else 1
+        self.ways = (tuple(range(self.levels)), tuple(reversed(range(self.levels))))[: self.orders]
+        self.piece = width // (replicas * self.orders)
+        self.width = width
+
+    def flip(self, rep, bit):
+        return rep + (1 << bit) * (1 - 2 * lax.rem(lax.div(rep, 1 << bit), 2))
+
+    def with_bits(self, rep, bits, number):
+        for at, bit in enumerate(bits):
+            had = lax.rem(lax.div(rep, 1 << bit), 2)
+            rep = rep + (1 << bit) * (((number >> at) & 1) - had)
+        return rep
+
+    def column(self, rep, order):
+        return pl.multiple_of((rep * self.orders + order) * self.piece, LANES)
+
+    def grow(self, rep, order, step):
+        bits = self.ways[order][:step]
+        return [self.with_bits(rep, bits, number) for number in range(1 << step)]
+
+    def grow_at(self, step):
+        return (1 << step) - 1
+
+    def halve(self, rep, order, step):
+        bits = self.ways[order][step + 1 :]
+        return [self.with_bits(rep, bits, number) for number in range(1 << len(bits))]
+
+    def halve_at(self, step):
+        return sum(1 << (self.levels - 1 - at) for at in range(step))
+
+
+def peer(rep, shard):
+    return {"rep": rep, "shard": shard}
+
+
+def remote(src, dst, send, recv, rep, shard):
+    return pltpu.make_async_remote_copy(
+        src_ref=src,
+        dst_ref=dst,
+        send_sem=send,
+        recv_sem=recv,
+        device_id=peer(rep, shard),
+        device_id_type=MESH,
+    )
+
+
+def greet_all(plan, rep, shard):
+    barrier = pltpu.get_barrier_semaphore()
+    total = plan.replicas * plan.shards
+
+    def hello(step, carry):
+        other = lax.rem(rep * plan.shards + shard + step, total)
+        pl.semaphore_signal(
+            barrier,
+            inc=1,
+            device_id=peer(lax.div(other, plan.shards), lax.rem(other, plan.shards)),
+            device_id_type=MESH,
+        )
+        return carry
+
+    lax.fori_loop(1, total, hello, 0)
+    pl.semaphore_wait(barrier, total - 1)
+
+
+def greet_near(plan, rep, shard):
+    barrier = pltpu.get_barrier_semaphore()
+    for step in range(1, plan.shards):
+        pl.semaphore_signal(
+            barrier,
+            inc=1,
+            device_id=peer(rep, lax.rem(shard + step, plan.shards)),
+            device_id_type=MESH,
+        )
+    for bit in range(plan.levels):
+        pl.semaphore_signal(
+            barrier, inc=1, device_id=peer(plan.flip(rep, bit), shard), device_id_type=MESH
+        )
+    pl.semaphore_wait(barrier, plan.shards - 1 + plan.levels)
+
+
+def gather_kernel(plan, *refs):
+    own, small = refs[:4], refs[4]
+    full, small_all = refs[5:9], refs[9]
+    stages = refs[10:14]
+    (load_sem, store_sem, small_send, small_recv, z_send, z_recv, rep_send, rep_recv, core_send,
+     core_recv) = refs[14:]
+    rep, shard = lax.axis_index("rep"), lax.axis_index("shard")
+    chips, piece = plan.chips, plan.piece
+    place, core = lax.div(shard, 2), lax.rem(shard, 2)
+    mate = place * 2 + (1 - core)
+    rows = own[0].shape[0]
+
+    def part(ref, mat, top, section_rep, order):
+        if mat < 3:
+            return ref.at[
+                pl.ds(pl.multiple_of(top, 8), rows),
+                pl.ds(plan.column(section_rep, order), piece),
+            ]
+        per = own[3].shape[1] // piece
+        section = section_rep * plan.orders + order
+        return ref.at[
+            pl.ds(pl.multiple_of(top + lax.div(section, per) * rows, 8), rows),
+            pl.ds(pl.multiple_of(lax.rem(section, per) * piece, LANES), piece),
+        ]
+
+    def slab_part(mat, slab, section_rep, order):
+        return part(full[mat], mat, slab * own[mat].shape[0], section_rep, order)
+
+    def slab_of(mat, slab):
+        deep = own[mat].shape[0]
+        return full[mat].at[pl.ds(pl.multiple_of(slab * deep, 8), deep), :]
+
+    sent = []
+
+    def launch(copy):
+        copy.start()
+        sent.append(copy)
+
+    loads = [pltpu.make_async_copy(own[mat], stages[mat], load_sem.at[mat]) for mat in range(4)]
+    for load in loads:
+        load.start()
+    small_all[shard] = small[...]
+    greet_near(plan, rep, shard)
+
+    def small_copy(step):
+        return remote(
+            small, small_all.at[shard], small_send.at[step - 1], small_recv.at[step - 1],
+            rep, lax.rem(shard + step, plan.shards),
+        )
+
+    for mat in range(4):
+        for gap in range(1, chips):
+            target = lax.rem(place - gap + chips, chips) * 2 + core
+            for order in range(plan.orders):
+                launch(remote(
+                    part(own[mat], mat, 0, rep, order),
+                    slab_part(mat, shard, rep, order),
+                    z_send.at[mat, gap - 1, order],
+                    z_recv.at[mat, gap - 1, order],
+                    rep, target,
+                ))
+        launch(remote(
+            own[mat], slab_of(mat, shard), core_send.at[mat, 0], core_recv.at[mat, 0], rep, mate
+        ))
+        if mat == 0:
+            for step in range(1, plan.shards):
+                launch(small_copy(step))
+
+    stores = []
+    for mat in range(4):
+        loads[mat].wait()
+        store = pltpu.make_async_copy(stages[mat], slab_of(mat, shard), store_sem.at[mat])
+        store.start()
+        stores.append(store)
+
+    def source(gap):
+        return lax.rem(place + gap, chips) * 2 + core
+
+    def exchange(mat, gap, order, step):
+        slab = source(gap)
+        far = plan.flip(rep, plan.ways[order][step])
+        at = plan.grow_at(step)
+        return [
+            remote(
+                slab_part(mat, slab, section, order),
+                slab_part(mat, slab, section, order),
+                rep_send.at[mat, gap - 1, order, at + number],
+                rep_recv.at[mat, gap - 1, order, at + number],
+                far, shard,
+            )
+            for number, section in enumerate(plan.grow(rep, order, step))
+        ]
+
+    def await_exchange(mat, gap, order, step):
+        slab = source(gap)
+        far = plan.flip(rep, plan.ways[order][step])
+        at = plan.grow_at(step)
+        for number, section in enumerate(plan.grow(far, order, step)):
+            there = slab_part(mat, slab, section, order)
+            remote(
+                there, there,
+                rep_send.at[mat, gap - 1, order, at + number],
+                rep_recv.at[mat, gap - 1, order, at + number],
+                far, shard,
+            ).wait_recv()
+
+    def relay(mat, gap, step):
+        for order in range(plan.orders):
+            if step == 0:
+                there = slab_part(mat, source(gap), rep, order)
+                remote(
+                    there, there, z_send.at[mat, gap - 1, order], z_recv.at[mat, gap - 1, order],
+                    rep, source(gap),
+                ).wait_recv()
+            else:
+                await_exchange(mat, gap, order, step - 1)
+            if step < plan.levels:
+                for copy in exchange(mat, gap, order, step):
+                    launch(copy)
+        if step == plan.levels:
+            there = slab_of(mat, source(gap))
+            launch(remote(
+                there, there, core_send.at[mat, gap], core_recv.at[mat, gap], rep, mate
+            ))
+
+    items = [(mat, gap) for mat in range(4) for gap in range(1, chips)]
+    for tick in range(len(items) + plan.levels):
+        for step in reversed(range(plan.levels + 1)):
+            if 0 <= tick - step < len(items):
+                relay(*items[tick - step], step)
+    for mat in range(4):
+        stores[mat].wait()
+        for gap in range(chips):
+            there = slab_of(mat, lax.rem(place + gap, chips) * 2 + (1 - core))
+            remote(
+                there, there, core_send.at[mat, gap], core_recv.at[mat, gap], rep, mate
+            ).wait_recv()
+    for step in range(1, plan.shards):
+        small_copy(step).wait_recv()
+    for copy in sent:
+        copy.wait_send()
+
+
+def gather_weights(plan, own, small):
+    hbm = pl.BlockSpec(memory_space=pl.ANY)
+    vmem = pl.BlockSpec(memory_space=pltpu.VMEM)
+    dma = pltpu.SemaphoreType.DMA
+    shapes = [
+        jax.ShapeDtypeStruct((array.shape[0] * plan.shards, array.shape[1]), array.dtype)
+        for array in own
+    ]
+    gaps = plan.chips - 1
+    crossing = plan.replicas - 1
+    return pl.pallas_call(
+        functools.partial(gather_kernel, plan),
+        out_shape=shapes + [jax.ShapeDtypeStruct((plan.shards,) + small.shape, small.dtype)],
+        in_specs=[hbm] * 4 + [vmem],
+        out_specs=[hbm] * 4 + [vmem],
+        scratch_shapes=[pltpu.VMEM(array.shape, array.dtype) for array in own]
+        + [
+            dma((4,)),
+            dma((4,)),
+            dma((plan.shards - 1,)),
+            dma((plan.shards - 1,)),
+            dma((4, gaps, plan.orders)),
+            dma((4, gaps, plan.orders)),
+            dma((4, gaps, plan.orders, crossing)),
+            dma((4, gaps, plan.orders, crossing)),
+            dma((4, plan.chips)),
+            dma((4, plan.chips)),
+        ],
+        compiler_params=pltpu.CompilerParams(
+            collective_id=0, has_side_effects=True, vmem_limit_bytes=VMEM_LIMIT
+        ),
+        name="gather_weights",
+    )(*own, small)
+
+
+def sum_kernel(plan, order_of, *refs):
+    joined, mixing, gate, up, down, small = refs[:6]
+    outs, small_out = refs[6:10], refs[10]
+    (held, mate_in, rep_in, z_in, final, small_in, load_sem, out_sem, small_sem, mate_send,
+     mate_recv, rep_send, rep_recv, z_send, z_recv, last_send, last_recv) = refs[11:]
+    rep, shard = lax.axis_index("rep"), lax.axis_index("shard")
+    chips, piece = plan.chips, plan.piece
+    place, core = lax.div(shard, 2), lax.rem(shard, 2)
+    mate = place * 2 + (1 - core)
+    rows = held.shape[2]
+    total = plan.replicas * plan.shards
+    sent = []
+
+    def launch(copy):
+        copy.start()
+        sent.append(copy)
+
+    def fragments(mat, slab):
+        top = pl.multiple_of(slab * rows, 8)
+        if mat == 0:
+            wide = joined.shape[1]
+            return [
+                (joined.at[pl.ds(top, rows), :], 0, wide),
+                (mixing.at[pl.ds(top, rows), :], wide, mixing.shape[1]),
+            ]
+        if mat < 3:
+            return [((gate, up)[mat - 1].at[pl.ds(top, rows), :], 0, plan.width)]
+        wide = down.shape[1]
+        return [
+            (
+                down.at[
+                    pl.ds(pl.multiple_of(slab * (rows * (plan.width // wide)) + at * rows, 8), rows),
+                    :,
+                ],
+                at * wide,
+                wide,
+            )
+            for at in range(plan.width // wide)
+        ]
+
+    items = [(mat, gap) for mat in order_of for gap in list(range(1, chips)) + [0]]
+
+    def slab_at(gap, which):
+        return lax.rem(place + gap, chips) * 2 + which
+
+    for mat, gap in items:
+        for ref, left, wide in fragments(mat, slab_at(gap, core)):
+            pltpu.make_async_copy(
+                ref, held.at[mat, gap, :, pl.ds(left, wide)], load_sem.at[mat, gap]
+            ).start()
+
+    greet_all(plan, rep, shard)
+
+    for mat, gap in items:
+        for ref, left, wide in fragments(mat, slab_at(gap, 1 - core)):
+            remote(
+                ref, mate_in.at[mat, gap, :, pl.ds(left, wide)],
+                mate_send.at[mat, gap], mate_recv.at[mat, gap], rep, mate,
+            ).start()
+
+    def small_go(step, carry):
+        other = lax.rem(rep * plan.shards + shard + step, total)
+        other_rep, other_shard = lax.div(other, plan.shards), lax.rem(other, plan.shards)
+        remote(
+            small.at[other_shard], small_in.at[step - 1], small_sem.at[0], small_sem.at[1],
+            other_rep, other_shard,
+        ).start()
+        return carry
+
+    lax.fori_loop(1, total, small_go, 0)
+
+    def whole_mate(mat, gap):
+        return remote(
+            mate_in.at[mat, gap], mate_in.at[mat, gap],
+            mate_send.at[mat, gap], mate_recv.at[mat, gap], rep, mate,
+        )
+
+    def cross(mat, gap, order, step):
+        far = plan.flip(rep, plan.ways[order][step])
+        at = plan.halve_at(step)
+        copies = [
+            remote(
+                held.at[mat, gap, :, pl.ds(plan.column(section, order), piece)],
+                rep_in.at[mat, gap, order, at + number],
+                rep_send.at[mat, gap, order, at + number],
+                rep_recv.at[mat, gap, order, at + number],
+                far, shard,
+            )
+            for number, section in enumerate(plan.halve(far, order, step))
+        ]
+        return copies, [plan.column(section, order) for section in plan.halve(rep, order, step)]
+
+    def last_piece(ref_at, order=None):
+        wide = plan.orders * piece
+        return ref_at, pl.ds(pl.multiple_of(rep * wide, LANES), wide)
+
+    def z_copy(mat, gap):
+        wide = plan.orders * piece
+        return remote(
+            held.at[mat, gap, :, pl.ds(pl.multiple_of(rep * wide, LANES), wide)],
+            z_in.at[mat, gap - 1],
+            z_send.at[mat, gap - 1], z_recv.at[mat, gap - 1],
+            rep, slab_at(gap, core),
+        )
+
+    def advance(mat, gap, step):
+        if step == 0:
+            pltpu.make_async_copy(
+                held.at[mat, gap], held.at[mat, gap], load_sem.at[mat, gap]
+            ).wait()
+            whole_mate(mat, gap).wait_recv()
+
+            def add(at, carry):
+                span = pl.ds(pl.multiple_of(at * piece, LANES), piece)
+                held[mat, gap, :, span] = (
+                    held[mat, gap, :, span].astype(jnp.float32)
+                    + mate_in[mat, gap, :, span].astype(jnp.float32)
+                ).astype(jnp.bfloat16)
+                return carry
+
+            lax.fori_loop(0, plan.width // piece, add, 0)
+        else:
+            for order in range(plan.orders):
+                copies, columns = cross(mat, gap, order, step - 1)
+                at = plan.halve_at(step - 1)
+                for number, (copy, column) in enumerate(zip(copies, columns)):
+                    copy.wait_recv()
+                    span = pl.ds(column, piece)
+                    held[mat, gap, :, span] = (
+                        held[mat, gap, :, span].astype(jnp.float32)
+                        + rep_in[mat, gap, order, at + number].astype(jnp.float32)
+                    ).astype(jnp.bfloat16)
+        if step < plan.levels:
+            for order in range(plan.orders):
+                for copy in cross(mat, gap, order, step)[0]:
+                    launch(copy)
+        elif gap > 0:
+            launch(z_copy(mat, gap))
+
+    def spread(mat, order, step):
+        far = plan.flip(rep, plan.ways[order][step])
+        at = plan.grow_at(step)
+        return [
+            remote(
+                final.at[mat, :, pl.ds(plan.column(section, order), piece)],
+                final.at[mat, :, pl.ds(plan.column(section, order), piece)],
+                last_send.at[mat, order, at + number],
+                last_recv.at[mat, order, at + number],
+                far, shard,
+            )
+            for number, section in enumerate(plan.grow(rep, order, step))
+        ]
+
+    def await_spread(mat, order, step):
+        far = plan.flip(rep, plan.ways[order][step])
+        at = plan.grow_at(step)
+        for number, section in enumerate(plan.grow(far, order, step)):
+            there = final.at[mat, :, pl.ds(plan.column(section, order), piece)]
+            remote(
+                there, there,
+                last_send.at[mat, order, at + number],
+                last_recv.at[mat, order, at + number],
+                far, shard,
+            ).wait_recv()
+
+    def finish(mat, step):
+        if step == 0:
+            for gap in range(1, chips):
+                z_copy(mat, gap).wait_recv()
+            for order in range(plan.orders):
+                span = pl.ds(plan.column(rep, order), piece)
+                here = pl.ds(order * piece, piece)
+                value = held[mat, 0, :, span].astype(jnp.float32)
+                for gap in range(1, chips):
+                    value = value + z_in[mat, gap - 1, :, here].astype(jnp.float32)
+                final[mat, :, span] = value.astype(jnp.bfloat16)
+        else:
+            for order in range(plan.orders):
+                await_spread(mat, order, step - 1)
+        if step < plan.levels:
+            for order in range(plan.orders):
+                for copy in spread(mat, order, step):
+                    launch(copy)
+        else:
+            pltpu.make_async_copy(final.at[mat], outs[mat], out_sem.at[mat]).start()
+
+    finals = []
+    for tick in range(len(items) + plan.levels):
+        for step in reversed(range(plan.levels + 1)):
+            if 0 <= tick - step < len(items):
+                advance(*items[tick - step], step)
+                if step == plan.levels and (tick - step) % chips == chips - 1:
+                    finals.append((items[tick - step][0], tick))
+        for mat, since in finals:
+            if tick > since and tick - since - 1 <= plan.levels:
+                finish(mat, tick - since - 1)
+    end = len(items) + plan.levels
+    for tick in range(end, end + plan.levels + 1):
+        for mat, since in finals:
+            if tick > since and tick - since - 1 <= plan.levels:
+                finish(mat, tick - since - 1)
+
+    everything = remote(small_in, small_in, small_sem.at[0], small_sem.at[1], rep, mate)
+    everything.wait_recv()
+
+    def gain(at, value):
+        return value + small_in[at]
+
+    small_out[...] = lax.fori_loop(0, total - 1, gain, small[shard])
+    everything.wait_send()
+    for mat, gap in items:
+        whole_mate(mat, gap).wait_send()
+    for copy in sent:
+        copy.wait_send()
+    for mat in order_of:
+        pltpu.make_async_copy(final.at[mat], outs[mat], out_sem.at[mat]).wait()
+
+
+def sum_grads(plan, grads, small):
+    hbm = pl.BlockSpec(memory_space=pl.ANY)
+    vmem = pl.BlockSpec(memory_space=pltpu.VMEM)
+    dma = pltpu.SemaphoreType.DMA
+    chips, gaps, crossing = plan.chips, plan.chips - 1, plan.replicas - 1
+    rows = grads[0].shape[0] // plan.shards
+    low = jnp.bfloat16
+    total = plan.replicas * plan.shards
+    return pl.pallas_call(
+        functools.partial(sum_kernel, plan, (3, 1, 2, 0)),
+        out_shape=[jax.ShapeDtypeStruct((rows, plan.width), low)] * 4
+        + [jax.ShapeDtypeStruct(small.shape[1:], small.dtype)],
+        in_specs=[hbm] * 5 + [vmem],
+        out_specs=[hbm] * 4 + [vmem],
+        scratch_shapes=[
+            pltpu.VMEM((4, chips, rows, plan.width), low),
+            pltpu.VMEM((4, chips, rows, plan.width), low),
+            pltpu.VMEM((4, chips, plan.orders, crossing, rows, plan.piece), low),
+            pltpu.VMEM((4, gaps, rows, plan.orders * plan.piece), low),
+            pltpu.VMEM((4, rows, plan.width), low),
+            pltpu.VMEM((total - 1,) + small.shape[1:], small.dtype),
+            dma((4, chips)),
+            dma((4,)),
+            dma((2,)),
+            dma((4, chips)),
+            dma((4, chips)),
+            dma((4, chips, plan.orders, crossing)),
+            dma((4, chips, plan.orders, crossing)),
+            dma((4, gaps)),
+            dma((4, gaps)),
+            dma((4, plan.orders, crossing)),
+            dma((4, plan.orders, crossing)),
+        ],
+        compiler_params=pltpu.CompilerParams(
+            collective_id=1, has_side_effects=True, vmem_limit_bytes=VMEM_LIMIT
+        ),
+        name="sum_grads",
+    )(*grads, small)
 
 
 def rotation(positions):
@@ -72,19 +599,25 @@
     positions,
     cotangent,
 ):
-    joined_full, mixing_full, innergain_full, innershift_full = (
-        lax.all_gather(joined_weight, "shard", axis=0, tiled=True),
-        lax.all_gather(mixing_weight, "shard", axis=0, tiled=True),
-        lax.all_gather(inner_gain, "shard", axis=0, tiled=True),
-        lax.all_gather(inner_shift, "shard", axis=0, tiled=True),
-    )
-    gate_full, upward_full, down_full, outergain_full, outershift_full = (
-        lax.all_gather(gate_weight, "shard", axis=0, tiled=True),
-        lax.all_gather(up_weight, "shard", axis=0, tiled=True),
-        lax.all_gather(down_weight, "shard", axis=0, tiled=True),
-        lax.all_gather(outer_gain, "shard", axis=0, tiled=True),
-        lax.all_gather(outer_shift, "shard", axis=0, tiled=True),
-    )
+    replicas, shards = lax.axis_size("rep"), lax.axis_size("shard")
+    plan = Plan(gate_weight.shape[1], replicas, shards)
+    part_rows = joined_weight.shape[0]
+    own_vectors = jnp.stack([inner_gain, inner_shift, outer_gain, outer_shift]).astype(jnp.float32)
+    own_vectors = jnp.pad(own_vectors, ((0, 4), (0, LANES - part_rows)))
+    attention_full, gate_full, upward_full, down_full, vectors = gather_weights(
+        plan,
+        (
+            jnp.concatenate([joined_weight, mixing_weight], axis=1),
+            gate_weight,
+            up_weight,
+            down_weight,
+        ),
+        own_vectors,
+    )
+    joined_full = attention_full[:, : joined_weight.shape[1]]
+    mixing_full = attention_full[:, joined_weight.shape[1] :]
+    vectors = vectors[:, :4, :part_rows].transpose(1, 0, 2).reshape(4, shards * part_rows)
+    innergain_full, innershift_full, outergain_full, outershift_full = vectors
     length = tokens.shape[0]
     model_width = tokens.shape[1]
     group_size = 4
@@ -154,11 +687,7 @@
         outershift_full.astype(jnp.float32),
     )
     layer_output = final.astype(jnp.bfloat16)
-    gate_back, upward_back, down_back = (
-        lax.all_gather(gate_weight, "shard", axis=0, tiled=True),
-        lax.all_gather(up_weight, "shard", axis=0, tiled=True),
-        lax.all_gather(down_weight, "shard", axis=0, tiled=True),
-    )
+    gate_back, upward_back, down_back = gate_full, upward_full, down_full
     outer_grad, outergain_grad, outershift_grad = outer_pull(cotangent.astype(jnp.float32))
     result_grad = outer_grad.astype(jnp.bfloat16)
     down_grad = token_contract(active_low, result_grad)
@@ -174,33 +703,7 @@
         + transposed_product(upward_low, upward_back)
     )
     inner_grad, innergain_grad, innershift_grad = inner_pull(normed_grad)
-    dense_sums = (
-        lax.psum_scatter(
-            gate_grad.astype(jnp.bfloat16), "shard", scatter_dimension=0, tiled=True
-        ).astype(jnp.float32),
-        lax.psum_scatter(
-            up_grad.astype(jnp.bfloat16), "shard", scatter_dimension=0, tiled=True
-        ).astype(jnp.float32),
-        lax.psum_scatter(
-            down_grad.astype(jnp.bfloat16), "shard", scatter_dimension=0, tiled=True
-        ).astype(jnp.float32),
-        lax.psum_scatter(
-            outergain_grad.astype(jnp.bfloat16), "shard", scatter_dimension=0, tiled=True
-        ).astype(jnp.float32),
-        lax.psum_scatter(
-            outershift_grad.astype(jnp.bfloat16), "shard", scatter_dimension=0, tiled=True
-        ).astype(jnp.float32),
-        lax.psum_scatter(
-            innergain_grad.astype(jnp.bfloat16), "shard", scatter_dimension=0, tiled=True
-        ).astype(jnp.float32),
-        lax.psum_scatter(
-            innershift_grad.astype(jnp.bfloat16), "shard", scatter_dimension=0, tiled=True
-        ).astype(jnp.float32),
-    )
-    joined_back, mixing_back = (
-        lax.all_gather(joined_weight, "shard", axis=0, tiled=True),
-        lax.all_gather(mixing_weight, "shard", axis=0, tiled=True),
-    )
+    joined_back, mixing_back = joined_full, mixing_full
     branch_grad = inner_grad.astype(jnp.bfloat16)
     mixing_grad = token_contract(attended_low, branch_grad)
     attended_grad = transposed_product(branch_grad, mixing_back).astype(jnp.bfloat16)
@@ -246,37 +749,35 @@
     ).astype(jnp.bfloat16)
     input_grad = (inner_grad + transposed_product(joined_low, joined_back)).astype(jnp.bfloat16)
     joined_grad = token_contract(tokens, joined_low)
-    mixer_sums = (
-        lax.psum_scatter(
-            joined_grad.astype(jnp.bfloat16), "shard", scatter_dimension=0, tiled=True
-        ).astype(jnp.float32),
-        lax.psum_scatter(
-            mixing_grad.astype(jnp.bfloat16), "shard", scatter_dimension=0, tiled=True
-        ).astype(jnp.float32),
-    )
-    summed = (
-        lax.psum(mixer_sums[0].astype(jnp.bfloat16), "rep").astype(jnp.float32),
-        lax.psum(mixer_sums[1].astype(jnp.bfloat16), "rep").astype(jnp.float32),
-        lax.psum(dense_sums[0].astype(jnp.bfloat16), "rep").astype(jnp.float32),
-        lax.psum(dense_sums[1].astype(jnp.bfloat16), "rep").astype(jnp.float32),
-        lax.psum(dense_sums[2].astype(jnp.bfloat16), "rep").astype(jnp.float32),
-        lax.psum(dense_sums[3].astype(jnp.bfloat16), "rep").astype(jnp.float32),
-        lax.psum(dense_sums[4].astype(jnp.bfloat16), "rep").astype(jnp.float32),
-        lax.psum(dense_sums[5].astype(jnp.bfloat16), "rep").astype(jnp.float32),
-        lax.psum(dense_sums[6].astype(jnp.bfloat16), "rep").astype(jnp.float32),
-    )
+    small = jnp.stack([innergain_grad, innershift_grad, outergain_grad, outershift_grad])
+    small = small.reshape(4, shards, part_rows).transpose(1, 0, 2)
+    small = jnp.pad(small, ((0, 0), (0, 4), (0, LANES - part_rows)))
+    low = jnp.bfloat16
+    attention_sum, gate_sum, up_sum, down_sum, small_sum = sum_grads(
+        plan,
+        (
+            joined_grad.astype(low),
+            mixing_grad.astype(low),
+            gate_grad.astype(low),
+            up_grad.astype(low),
+            down_grad.astype(low),
+        ),
+        small,
+    )
+    down_sum = down_sum.reshape(part_rows, -1, model_width).transpose(1, 0, 2)
+    full = jnp.float32
     return (
         layer_output,
         input_grad,
-        summed[0],
-        summed[1],
-        summed[2],
-        summed[3],
-        summed[4],
-        summed[7],
-        summed[8],
-        summed[5],
-        summed[6],
+        attention_sum[:, : joined_weight.shape[1]].astype(full),
+        attention_sum[:, joined_weight.shape[1] :].astype(full),
+        gate_sum.astype(full),
+        up_sum.astype(full),
+        down_sum.reshape(down_weight.shape).astype(full),
+        small_sum[0, :part_rows],
+        small_sum[1, :part_rows],
+        small_sum[2, :part_rows],
+        small_sum[3, :part_rows],
     )
 
 

time: 660 us -> 368 us (0.56)
  waiting for transfers between devices: 402 us -> 0 us
  Pallas kernels: 0 us -> 229 us
  blocking collectives: 55.8 us -> 0 us
  matrix products: 120 us -> 86.7 us
  local copies, waits for them, and re-layouts: 29.5 us -> 14.6 us
  between operations: 16.1 us -> 1.44 us
    pallas_call x0 -> x2, Pallas kernels: none -> 229 us  [the longest x1 123 us: sum_grads(): pl.pallas_call(functools.partial(sum_kernel, plan, (3, 1, 2, 0)), out_sha...]
    reduce_scatter x4 -> x0, waiting for transfers between devices: 199 us -> none  [the longest x1 55.7 us: on_device(): lax.psum_scatter(gate_grad.astype(jnp.bfloat16), 'shard', scatter_dimensi...]
    all_gather x5 -> x0, waiting for transfers between devices: 150 us -> none  [the longest x1 43.6 us: on_device(): lax.all_gather(up_weight, 'shard', axis=0, tiled=True)]
    unnamed x2 -> x0, blocking collectives: 45.1 us -> none
    psum x1 -> x0, waiting for transfers between devices: 32 us -> none  [on_device(): lax.psum(mixer_sums[0].astype(jnp.bfloat16), 'rep').astype(jnp.float32)]
    unnamed x12 -> x0, waiting for transfers between devices: 21.2 us -> none
    unnamed x96 -> x84, local copies, waits for them, and re-layouts: 19.2 us -> 5.22 us
    psum x1 -> x0, blocking collectives: 10.7 us -> none  [on_device(): lax.psum(dense_sums[5].astype(jnp.bfloat16), 'rep').astype(jnp.float32)]
  transfers between devices with their start and end apart: 11 -> 0, of which waited for: 10 -> 0; matrix products, arithmetic and copies ran while one was open for 13% -> 0% of each run, Pallas kernels for 0% -> 0%
where the time goes in v1:
time: 368 us; the launch traced here: 363 us
  Pallas kernels  229 us (62%)
  matrix products  86.7 us (24%)
  other arithmetic  30.4 us (8%)
  local copies, waits for them, and re-layouts  14.6 us (4%)
    pallas_call x1, Pallas kernels, sum_grads(): pl.pallas_call(functools.partial(sum_kernel, plan, (3, 1, 2, 0)), out_sha...  123 us
    pallas_call x1, Pallas kernels, gather_weights(): pl.pallas_call(functools.partial(gather_kernel, plan), out_shape=shapes +...  106 us
    dot_general x5, matrix products, transposed_product(): lax.dot_general(left, right, (((1,), (1,)), ((), ())), preferred_element_...  21.8 us
    dot_general x5, matrix products, token_contract(): lax.dot_general(left, right, (((0,), (0,)), ((), ())), preferred_element_...  19.2 us
    dot_general x3, matrix products, head_backward(): jnp.einsum('hqd,hkd->hqk', output_block, value_block, preferred_element_t...  7.39 us

profile of v1, /device:TPU:0, one launch (start us, length us, event | category | flops | bytes accessed | tf_op | source)
XLA Modules:
  0.0 362.8 jit_solution(11105217600886364255)
XLA Ops:
  0.7 2.0 pad_maximum_fusion.3.refs_0_
  2.7 1.3 fusion.94.refs_4_
  4.0 105.8 %gather_weights.1 = (bf16[768,3072]{1,0:T(8,128)(2,1)}, bf16[768,3072]{1,0:T(8,128)(2,1)}, bf16[768,3072]{1,0:T(8,128)(2,1)}, bf16[3072,768]{1,0:T(8,128)(2,1)}, f32[8,8,128]{2,1,0:T(8,128)}) custom-call(bf16[96,3072]{1,0:T(8,128)(2,1)} %pad_maximum_fusion.3.refs_0_, bf16[96,3072]{1,0:T(8,128)(2,1)} %refs_1_.1, bf16[96,3072]{1,0:T(8,128)(2,1)} %refs_2_.1, ...), custom_call_target="tpu_custom_call" | custom-call | tf_op jit(solution)/shard_map/gather_weights/pallas_call | solution.py:260
  109.8 4.1 %convolution_bitcast_fusion = f32[512,2304]{0,1:T(8,128)S(1)} fusion(bf16[512,768]{1,0:T(8,128)(2,1)S(1)} %copy-done.21, bf16[768,3072]{1,0:T(8,128)(2,1)} %get-tuple-element.113), kind=kOutput, calls=%fused_computation.75 | convolution fusion | flops 1811939328 | bytes 9043968 | tf_op jit(solution)/shard_map/dot_general | solution.py:627
  115.3 0.9 fusion.73
  116.5 10.7 %while.28 = (s32[]{:T(128)}, bf16[3,4,512,64]{2,3,1,0:T(8,128)(2,1)S(1)}, f32[3,4,512,1]{2,1,3,0:T(4,128)S(1)}, bf16[3,4,512,64]{2,3,1,0:T(8,128)(2,1)S(1)}, bf1...) while((s32[]{:T(128)}, ...), condition=%wide.region_3.4_spmd.clone, body=%wide.region_0.3_spmd.clone.sunk | while | flops 281409536 | bytes 14749793 | solution.py:665
  117.0 0.9 fusion.151
  118.0 0.9 fusion.152
  118.9 1.4 fusion.153
  120.5 0.9 fusion.151
  121.4 0.9 fusion.152
  122.3 1.4 fusion.153
  124.0 0.9 fusion.151
  124.9 0.9 fusion.152
  125.8 1.4 fusion.153
  127.2 0.9 copy-done.3
  128.4 2.6 fusion.108
  131.9 4.9 %fusion.110 = f32[512,3072]{1,0:T(8,128)S(1)} fusion(bf16[512,768]{1,0:T(8,128)(2,1)S(1)} %fusion.80, bf16[768,3072]{1,0:T(8,128)(2,1)} %get-tuple-element.116), kind=kOutput, calls=%fused_computation.181 | convolution fusion | flops 2415919104 | bytes 11796480 | tf_op jit(solution)/shard_map/dot_general | solution.py:676
  136.9 5.0 %multiply_convert_fusion.2 = (bf16[512,3072]{1,0:T(8,128)(2,1)S(1)}, f32[512,3072]{1,0:T(8,128)}) fusion(f32[512,3072]{1,0:T(8,128)S(1)} %fusion.110, bf16[512,768]{1,0:T(8,128)(2,1)S(1)} %fusion.80, bf16[768,3072]{1,0:T(8,128)(2,1)S(1)} %bitcast.218), kind=kOutput, calls=%fused_computation.68 | convolution fusion | flops 2425356288 | bytes 21233664 | tf_op jit(solution)/shard_map/dot_general | solution.py:677
  141.9 2.7 fusion.109
  144.6 1.1 copy-done
  146.2 2.3 fusion.69
  148.6 3.3 fusion.104
  151.9 9.4 %multiply_convert_fusion.1 = (bf16[512,3072]{1,0:T(8,128)(2,1)S(1)}, bf16[512,3072]{1,0:T(8,128)(2,1)S(1)}) fusion(f32[512,3072]{1,0:T(8,128)} %copy-done.1, f32[512,3072]{1,0:T(8,128)} %get-tuple-element.248, bf16[3072,768]{1,0:T(8,128)(2,1)} %get-tuple-element.118, f32[512,768]{1,0:T(8,128)S(1)} %get-tuple-element.215, f32[512]{0:T(512)S(1)} %negate_multiply_fusion.1), kind=kOutput, calls=%fused_computation.67 | convolution fusion | flops 2438725632 | bytes 25167872 | tf_op jit(solution)/shard_map/dot_general | solution.py:564
  161.3 2.7 fusion.111
  164.1 3.2 multiply_reduce_fusion.1
  167.3 1.7 fusion.103
  169.0 3.5 convolution_convert_fusion.5
  172.5 2.3 copy.35
  174.8 27.3 %while.29 = (s32[]{:T(128)}, f32[3,4,512,64]{2,3,1,0:T(8,128)S(1)}, f32[3,4,512,64]{2,3,1,0:T(8,128)}, bf16[3,4,512,64]{2,3,1,0:T(8,128)(2,1)}, bf16[3,4,512,64]...) while((s32[]{:T(128)}, f32[3,4,512,64]{2,3,1,0:T(8,128)S(1)}, ...), condition=%wide.region_14.15_spmd.clone, body=%wide.region_12.14_spmd.clone.sunk | while | flops 687339520 | bytes 45415628 | solution.py:735
  174.9 0.8 fusion.162
  176.1 2.5 multiply_reduce_fusion.6
  178.5 1.3 multiply_convert_fusion.4
  180.3 1.6 fusion.164
  181.8 1.2 fusion.165
  183.1 0.9 copy-done.27
  183.9 0.8 fusion.162
  185.1 2.5 multiply_reduce_fusion.6
  187.5 1.3 multiply_convert_fusion.4
  189.3 1.6 fusion.164
  190.8 1.2 fusion.165
  192.1 0.9 copy-done.27
  193.0 0.8 fusion.162
  194.1 2.5 multiply_reduce_fusion.6
  196.6 1.3 multiply_convert_fusion.4
  198.3 1.6 fusion.164
  199.9 1.2 fusion.165
  201.1 0.9 copy-done.27
  202.0 1.9 bitcast_multiply_fusion.2
  204.3 1.2 copy-done.2
  205.5 0.9 fusion.77
  207.2 3.0 add_convert_fusion
  210.2 3.8 %fusion.62.refs_0_ = bf16[768,2304]{1,0:T(8,128)(2,1)} fusion(bf16[512,768]{1,0:T(8,128)(2,1)S(1)} %copy-done.22, bf16[512,768]{0,1:T(8,128)(2,1)S(1)} %bitcast.226, bf16[512,768]{0,1:T(8,128)(2,1)S(1)} %bitcast.209, bf16[512,768]{0,1:T(8,128)(2,1)S(1)} %bitcast.207), kind=kOutput, calls=%fused_computation.76 | convolution fusion | flops 1820786688 | bytes 6684672 | tf_op jit(solution)/shard_map/dot_general | solution.py:570
  214.1 1.9 convolution_convert_fusion.4.refs_1_
  216.0 0.6 copy-done.32
  216.6 4.6 %convolution_convert_fusion.2.refs_2_ = bf16[768,3072]{1,0:T(8,128)(2,1)} fusion(bf16[512,768]{1,0:T(8,128)(2,1)S(1)} %copy-done.6, bf16[512,3072]{1,0:T(8,128)(2,1)S(1)} %copy-done.32), kind=kOutput, calls=%fused_computation.73 | convolution fusion | flops 2418278400 | bytes 8650752 | tf_op jit(solution)/shard_map/dot_general | solution.py:570
  221.2 4.4 %convolution_convert_fusion.1.refs_3_ = bf16[768,3072]{1,0:T(8,128)(2,1)} fusion(bf16[512,768]{1,0:T(8,128)(2,1)S(1)} %copy-done.6, bf16[512,3072]{1,0:T(8,128)(2,1)S(1)} %copy-done.30), kind=kOutput, calls=%fused_computation.72 | convolution fusion | flops 2418278400 | bytes 8650752 | tf_op jit(solution)/shard_map/dot_general | solution.py:570
  225.6 4.5 %convolution_convert_fusion.refs_4_ = bf16[3072,768]{1,0:T(8,128)(2,1)} fusion(bf16[512,3072]{1,0:T(8,128)(2,1)S(1)} %copy-done.34, f32[512,768]{1,0:T(8,128)S(1)} %copy-done.8, f32[512]{0:T(512)S(1)} %negate_multiply_fusion.1), kind=kOutput, calls=%fused_computation.71 | convolution fusion | flops 2419064832 | bytes 9439232 | tf_op jit(solution)/shard_map/dot_general | solution.py:570
  231.1 123.2 %sum_grads.1 = (bf16[96,3072]{1,0:T(8,128)(2,1)}, bf16[96,3072]{1,0:T(8,128)(2,1)}, bf16[96,3072]{1,0:T(8,128)(2,1)}, bf16[96,3072]{1,0:T(8,128)(2,1)}, f32[8,128]{1,0:T(8,128)}) custom-call(bf16[768,2304]{1,0:T(8,128)(2,1)} %fusion.62.refs_0_, bf16[768,768]{1,0:T(8,128)(2,1)} %convolution_convert_fusion.4.refs_1_, ...), custom_call_target="tpu_custom_call" | custom-call | tf_op jit(solution)/shard_map/sum_grads/pallas_call | solution.py:511
  354.3 2.1 slice_convert_fusion.1
  356.4 1.7 slice_convert_fusion.2
  358.1 1.1 convert_element_type.132
  359.2 1.1 convert_element_type.133
  360.9 1.2 copy.37
  (154 shorter events, 9.5 us)
Async XLA Ops:
  0.6 109.2 %copy-start.21 = (bf16[512,768]{1,0:T(8,128)(2,1)S(1)}, bf16[512,768]{1,0:T(8,128)(2,1)}, u32[]{:S(2)}) copy-start(bf16[512,768]{1,0:T(8,128)(2,1)} %param.17) | copy-start | bytes 2359300
  114.3 0.7 copy-start.19
  115.3 1.0 copy-start.10
  115.3 1.0 copy-start.12
  115.3 1.1 copy-start.14
  115.3 1.2 copy-start.23
  127.2 0.9 copy-start.3
  127.2 1.1 copy-start.24
  128.4 2.6 copy-start.18
  131.5 5.3 %slice-start.4 = ((s8[4718592]{0:T(1024)(128)(4,1)}), s8[4194304]{0:T(1024)(128)(4,1)S(1)}, s32[]{:S(2)}) async-start(s8[4718592]{0:T(1024)(128)(4,1)} %bitcast.217), calls=%async_computation.4 | async-start | bytes 8388608
  131.9 5.0 %copy-start.5 = (bf16[512,768]{1,0:T(8,128)(2,1)}, bf16[512,768]{1,0:T(8,128)(2,1)S(1)}, u32[]{:S(2)}) copy-start(bf16[512,768]{1,0:T(8,128)(2,1)S(1)} %fusion.80) | copy-start | bytes 2359300
  131.9 5.0 %slice-start.5 = ((s8[4718592]{0:T(1024)(128)(4,1)}), s8[524288]{0:T(1024)(128)(4,1)S(1)}, s32[]{:S(2)}) async-start(s8[4718592]{0:T(1024)(128)(4,1)} %bitcast.217), calls=%async_computation.5 | async-start | bytes 1048576
  131.9 10.0 %slice-start.8 = ((s8[4718592]{0:T(1024)(128)(4,1)}), s8[4194304]{0:T(1024)(128)(4,1)S(1)}, s32[]{:S(2)}) async-start(s8[4718592]{0:T(1024)(128)(4,1)} %bitcast.221), calls=%async_computation.8 | async-start | bytes 8388608
  136.8 5.0 %copy-start.1 = (f32[512,3072]{1,0:T(8,128)}, f32[512,3072]{1,0:T(8,128)S(1)}, u32[]{:S(2)}) copy-start(f32[512,3072]{1,0:T(8,128)S(1)} %fusion.110) | copy-start | bytes 18874372
  136.9 5.0 %slice-start.9 = ((s8[4718592]{0:T(1024)(128)(4,1)}), s8[524288]{0:T(1024)(128)(4,1)S(1)}, s32[]{:S(2)}) async-start(s8[4718592]{0:T(1024)(128)(4,1)} %bitcast.221), calls=%async_computation.9 | async-start | bytes 1048576
  141.9 2.8 copy-start.33
  144.6 1.1 copy-start
  148.5 12.8 %slice-start = ((s8[4718592]{0:T(1024)(128)(4,1)}), s8[4194304]{0:T(1024)(128)(4,1)S(1)}, s32[]{:S(2)}) async-start(s8[4718592]{0:T(1024)(128)(4,1)} %bitcast.202), calls=%async_computation | async-start | bytes 8388608
  148.5 15.5 %slice-start.6 = ((s8[4718592]{0:T(1024)(128)(4,1)}), s8[4194304]{0:T(1024)(128)(4,1)S(1)}, s32[]{:S(2)}) async-start(s8[4718592]{0:T(1024)(128)(4,1)} %bitcast.219), calls=%async_computation.6 | async-start | bytes 8388608
  151.9 12.1 %copy-start.7 = (f32[512,768]{1,0:T(8,128)}, f32[512,768]{1,0:T(8,128)S(1)}, u32[]{:S(2)}) copy-start(f32[512,768]{1,0:T(8,128)S(1)} %get-tuple-element.215) | copy-start | bytes 4718596
  151.9 9.4 %slice-start.1 = ((s8[4718592]{0:T(1024)(128)(4,1)}), s8[524288]{0:T(1024)(128)(4,1)S(1)}, s32[]{:S(2)}) async-start(s8[4718592]{0:T(1024)(128)(4,1)} %bitcast.202), calls=%async_computation.1 | async-start | bytes 1048576
  151.9 12.2 %slice-start.7 = ((s8[4718592]{0:T(1024)(128)(4,1)}), s8[524288]{0:T(1024)(128)(4,1)S(1)}, s32[]{:S(2)}) async-start(s8[4718592]{0:T(1024)(128)(4,1)} %bitcast.219), calls=%async_computation.7 | async-start | bytes 1048576
  161.3 2.7 copy-start.29
  161.3 2.8 copy-start.31
  174.8 27.3 %copy-start.13 = (f32[512,64]{0,1:T(8,128)S(1)}, f32[512,64]{0,1:T(8,128)}, u32[]{:S(2)}) copy-start(f32[512,64]{0,1:T(8,128)} %copy-done.12) | copy-start | bytes 393220
  174.9 1.1 copy-start.4
  180.2 1.6 copy-start.26
  183.1 0.9 copy-start.27
  183.9 1.1 copy-start.4
  189.3 1.6 copy-start.26
  192.1 0.9 copy-start.27
  193.0 1.1 copy-start.4
  198.3 1.6 copy-start.26
  201.1 0.9 copy-start.27
  202.0 4.4 %slice-start.2 = ((s8[4718592]{0:T(1024)(128)(4,1)}), s8[4194304]{0:T(1024)(128)(4,1)S(1)}, s32[]{:S(2)}) async-start(s8[4718592]{0:T(1024)(128)(4,1)} %bitcast.215), calls=%async_computation.2 | async-start | bytes 8388608
  204.1 1.4 copy-start.2
  204.1 1.4 copy-start.11
  204.1 2.3 slice-start.3
  205.5 1.4 copy-start.9
  205.5 1.6 copy-start.28
  207.2 3.0 copy-start.22
  210.2 3.8 %copy-start.25 = (bf16[3,4,512,64]{2,3,1,0:T(8,128)(2,1)S(1)}, bf16[3,4,512,64]{2,3,1,0:T(8,128)(2,1)}, u32[]{:S(2)}) copy-start(bf16[3,4,512,64]{2,3,1,0:T(8,128)(2,1)} %copy-done.24) | copy-start | bytes 2359300
  214.0 1.9 copy-start.6
  214.1 2.6 copy-start.32
  216.6 4.6 %copy-start.30 = (bf16[512,3072]{1,0:T(8,128)(2,1)S(1)}, bf16[512,3072]{1,0:T(8,128)(2,1)}, u32[]{:S(2)}) copy-start(bf16[512,3072]{1,0:T(8,128)(2,1)} %copy-done.29) | copy-start | bytes 9437188
  221.2 4.4 %copy-start.8 = (f32[512,768]{1,0:T(8,128)S(1)}, f32[512,768]{1,0:T(8,128)}, u32[]{:S(2)}) copy-start(f32[512,768]{1,0:T(8,128)} %copy-done.7) | copy-start | bytes 4718596
  221.2 4.4 %copy-start.34 = (bf16[512,3072]{1,0:T(8,128)(2,1)S(1)}, bf16[512,3072]{1,0:T(8,128)(2,1)}, u32[]{:S(2)}) copy-start(bf16[512,3072]{1,0:T(8,128)(2,1)} %copy-done.33) | copy-start | bytes 9437188
  354.3 3.8 %copy-start.17 = (bf16[96,3072]{1,0:T(8,128)(2,1)S(1)}, bf16[96,3072]{1,0:T(8,128)(2,1)}, u32[]{:S(2)}) copy-start(bf16[96,3072]{1,0:T(8,128)(2,1)} %get-tuple-element.124) | copy-start | bytes 1769476
  354.3 4.9 %copy-start.16 = (bf16[96,3072]{1,0:T(8,128)(2,1)S(1)}, bf16[96,3072]{1,0:T(8,128)(2,1)}, u32[]{:S(2)}) copy-start(bf16[96,3072]{1,0:T(8,128)(2,1)} %get-tuple-element.125) | copy-start | bytes 1769476
  356.3 3.9 %copy-start.15 = (bf16[96,3072]{1,0:T(8,128)(2,1)S(1)}, bf16[96,3072]{1,0:T(8,128)(2,1)}, u32[]{:S(2)}) copy-start(bf16[96,3072]{1,0:T(8,128)(2,1)} %get-tuple-element.126) | copy-start | bytes 1769476
  360.3 1.8 copy-start.20

commit v2 on v1

--- a/solution.py
+++ b/solution.py
@@ -16,6 +16,8 @@
 LANES = 128
 MESH = pl.DeviceIdType.MESH
 VMEM_LIMIT = 62 * 1024 * 1024
+SLACK = 2
+AHEAD = 3
 
 
 class Plan:
@@ -154,23 +156,27 @@
             rep, lax.rem(shard + step, plan.shards),
         )
 
+    items = [(mat, gap) for mat in range(4) for gap in range(1, chips)]
+
+    def along(mat, gap):
+        target = lax.rem(place - gap + chips, chips) * 2 + core
+        for order in range(plan.orders):
+            launch(remote(
+                part(own[mat], mat, 0, rep, order),
+                slab_part(mat, shard, rep, order),
+                z_send.at[mat, gap - 1, order],
+                z_recv.at[mat, gap - 1, order],
+                rep, target,
+            ))
+
+    for item in items[:AHEAD]:
+        along(*item)
+    for step in range(1, plan.shards):
+        launch(small_copy(step))
     for mat in range(4):
-        for gap in range(1, chips):
-            target = lax.rem(place - gap + chips, chips) * 2 + core
-            for order in range(plan.orders):
-                launch(remote(
-                    part(own[mat], mat, 0, rep, order),
-                    slab_part(mat, shard, rep, order),
-                    z_send.at[mat, gap - 1, order],
-                    z_recv.at[mat, gap - 1, order],
-                    rep, target,
-                ))
         launch(remote(
             own[mat], slab_of(mat, shard), core_send.at[mat, 0], core_recv.at[mat, 0], rep, mate
         ))
-        if mat == 0:
-            for step in range(1, plan.shards):
-                launch(small_copy(step))
 
     stores = []
     for mat in range(4):
@@ -229,11 +235,15 @@
                 there, there, core_send.at[mat, gap], core_recv.at[mat, gap], rep, mate
             ))
 
-    items = [(mat, gap) for mat in range(4) for gap in range(1, chips)]
-    for tick in range(len(items) + plan.levels):
-        for step in reversed(range(plan.levels + 1)):
-            if 0 <= tick - step < len(items):
-                relay(*items[tick - step], step)
+    events = [
+        (at + SLACK * step, -step, item, step)
+        for at, item in enumerate(items)
+        for step in range(plan.levels + 1)
+    ]
+    for at, _, item, step in sorted(events):
+        relay(*item, step)
+        if step == 0 and at + AHEAD < len(items):
+            along(*items[at + AHEAD])
     for mat in range(4):
         stores[mat].wait()
         for gap in range(chips):
@@ -468,21 +478,19 @@
         else:
             pltpu.make_async_copy(final.at[mat], outs[mat], out_sem.at[mat]).start()
 
-    finals = []
-    for tick in range(len(items) + plan.levels):
-        for step in reversed(range(plan.levels + 1)):
-            if 0 <= tick - step < len(items):
-                advance(*items[tick - step], step)
-                if step == plan.levels and (tick - step) % chips == chips - 1:
-                    finals.append((items[tick - step][0], tick))
-        for mat, since in finals:
-            if tick > since and tick - since - 1 <= plan.levels:
-                finish(mat, tick - since - 1)
-    end = len(items) + plan.levels
-    for tick in range(end, end + plan.levels + 1):
-        for mat, since in finals:
-            if tick > since and tick - since - 1 <= plan.levels:
-                finish(mat, tick - since - 1)
+    events = []
+    for at, item in enumerate(items):
+        for step in range(plan.levels + 1):
+            events.append((at + SLACK * step, -step, item[0], item[1], step))
+    for number, mat in enumerate(order_of):
+        since = (number + 1) * chips - 1 + SLACK * plan.levels
+        for step in range(plan.levels + 1):
+            events.append((since + SLACK * (step + 1), -plan.levels - 1 - step, mat, -1, step))
+    for _, _, mat, gap, step in sorted(events):
+        if gap < 0:
+            finish(mat, step)
+        else:
+            advance(mat, gap, step)
 
     everything = remote(small_in, small_in, small_sem.at[0], small_sem.at[1], rep, mate)
     everything.wait_recv()

time: 368 us -> 336 us (0.913)
  Pallas kernels: 229 us -> 196 us
    pallas_call x1, Pallas kernels: 106 us -> 83.9 us  [gather_weights(): pl.pallas_call(functools.partial(gather_kernel, plan), out_shape=shapes +...]
    pallas_call x1, Pallas kernels: 123 us -> 113 us  [sum_grads(): pl.pallas_call(functools.partial(sum_kernel, plan, (3, 1, 2, 0)), out_sha...]
where the time goes in v2:
time: 336 us; the launch traced here: 330 us
  Pallas kernels  196 us (58%)
  matrix products  86.7 us (26%)
  other arithmetic  30.4 us (9%)
  local copies, waits for them, and re-layouts  14.6 us (4%)
    pallas_call x1, Pallas kernels, sum_grads(): pl.pallas_call(functools.partial(sum_kernel, plan, (3, 1, 2, 0)), out_sha...  113 us
    pallas_call x1, Pallas kernels, gather_weights(): pl.pallas_call(functools.partial(gather_kernel, plan), out_shape=shapes +...  83.9 us
    dot_general x5, matrix products, transposed_product(): lax.dot_general(left, right, (((1,), (1,)), ((), ())), preferred_element_...  21.8 us
    dot_general x5, matrix products, token_contract(): lax.dot_general(left, right, (((0,), (0,)), ((), ())), preferred_element_...  19.2 us
    dot_general x3, matrix products, head_backward(): jnp.einsum('hqd,hkd->hqk', output_block, value_block, preferred_element_t...  7.39 us

profile of v2, /device:TPU:0, one launch (start us, length us, event | category | flops | bytes accessed | tf_op | source)
XLA Modules:
  0.0 330.3 jit_solution(7832767572807005247)
XLA Ops:
  0.7 2.0 pad_maximum_fusion.3.refs_0_
  2.7 1.3 fusion.94.refs_4_
  4.0 83.9 %gather_weights.1 = (bf16[768,3072]{1,0:T(8,128)(2,1)}, bf16[768,3072]{1,0:T(8,128)(2,1)}, bf16[768,3072]{1,0:T(8,128)(2,1)}, bf16[3072,768]{1,0:T(8,128)(2,1)}, f32[8,8,128]{2,1,0:T(8,128)}) custom-call(bf16[96,3072]{1,0:T(8,128)(2,1)} %pad_maximum_fusion.3.refs_0_, bf16[96,3072]{1,0:T(8,128)(2,1)} %refs_1_.1, bf16[96,3072]{1,0:T(8,128)(2,1)} %refs_2_.1, ...), custom_call_target="tpu_custom_call" | custom-call | tf_op jit(solution)/shard_map/gather_weights/pallas_call | solution.py:270
  87.9 4.1 %convolution_bitcast_fusion = f32[512,2304]{0,1:T(8,128)S(1)} fusion(bf16[512,768]{1,0:T(8,128)(2,1)S(1)} %copy-done.21, bf16[768,3072]{1,0:T(8,128)(2,1)} %get-tuple-element.113), kind=kOutput, calls=%fused_computation.75 | convolution fusion | flops 1811939328 | bytes 9043968 | tf_op jit(solution)/shard_map/dot_general | solution.py:635
  93.4 0.9 fusion.73
  94.6 10.7 %while.28 = (s32[]{:T(128)}, bf16[3,4,512,64]{2,3,1,0:T(8,128)(2,1)S(1)}, f32[3,4,512,1]{2,1,3,0:T(4,128)S(1)}, bf16[3,4,512,64]{2,3,1,0:T(8,128)(2,1)S(1)}, bf1...) while((s32[]{:T(128)}, ...), condition=%wide.region_3.4_spmd.clone, body=%wide.region_0.3_spmd.clone.sunk | while | flops 281409536 | bytes 14749793 | solution.py:673
  95.1 0.9 fusion.151
  96.0 0.9 fusion.152
  97.0 1.4 fusion.153
  98.6 0.9 fusion.151
  99.5 0.9 fusion.152
  100.4 1.4 fusion.153
  102.1 0.9 fusion.151
  103.0 0.9 fusion.152
  103.9 1.4 fusion.153
  105.3 0.9 copy-done.3
  106.5 2.6 fusion.108
  110.0 4.9 %fusion.110 = f32[512,3072]{1,0:T(8,128)S(1)} fusion(bf16[512,768]{1,0:T(8,128)(2,1)S(1)} %fusion.80, bf16[768,3072]{1,0:T(8,128)(2,1)} %get-tuple-element.116), kind=kOutput, calls=%fused_computation.181 | convolution fusion | flops 2415919104 | bytes 11796480 | tf_op jit(solution)/shard_map/dot_general | solution.py:684
  115.0 5.0 %multiply_convert_fusion.2 = (bf16[512,3072]{1,0:T(8,128)(2,1)S(1)}, f32[512,3072]{1,0:T(8,128)}) fusion(f32[512,3072]{1,0:T(8,128)S(1)} %fusion.110, bf16[512,768]{1,0:T(8,128)(2,1)S(1)} %fusion.80, bf16[768,3072]{1,0:T(8,128)(2,1)S(1)} %bitcast.218), kind=kOutput, calls=%fused_computation.68 | convolution fusion | flops 2425356288 | bytes 21233664 | tf_op jit(solution)/shard_map/dot_general | solution.py:685
  120.0 2.7 fusion.109
  122.7 1.1 copy-done
  124.2 2.3 fusion.69
  126.6 3.3 %fusion.104 = (f32[512]{0:T(512)S(1)}, f32[512,768]{1,0:T(8,128)S(1)}, bf16[512,768]{1,0:T(8,128)(2,1)}) fusion(f32[512]{0:T(512)S(1)} %multiply_multiply_fusion.1, f32[512,768]{1,0:T(8,128)} %copy-done, f32[512]{0:T(512)S(1)} %broadcast_multiply_fusion.1, f32[512]{0:T(512)S(1)} %fusion.99, f32[768]{0:T(1024)S(1)} %mul.275, bf16[512,768]{1,0:T(8,128)(2,1)} %param.29, ...), kind=kLoop, calls=%fused_computation.175 | loop fusion | flops 4718080 | bytes 4732928 | tf_op jit(solution)/shard_map/transpose(jvp())/reduce_sum | solution.py:566
  130.0 9.4 %multiply_convert_fusion.1 = (bf16[512,3072]{1,0:T(8,128)(2,1)S(1)}, bf16[512,3072]{1,0:T(8,128)(2,1)S(1)}) fusion(f32[512,3072]{1,0:T(8,128)} %copy-done.1, f32[512,3072]{1,0:T(8,128)} %get-tuple-element.248, bf16[3072,768]{1,0:T(8,128)(2,1)} %get-tuple-element.118, f32[512,768]{1,0:T(8,128)S(1)} %get-tuple-element.215, f32[512]{0:T(512)S(1)} %negate_multiply_fusion.1), kind=kOutput, calls=%fused_computation.67 | convolution fusion | flops 2438725632 | bytes 25167872 | tf_op jit(solution)/shard_map/dot_general | solution.py:572
  139.4 2.7 fusion.111
  142.2 3.2 multiply_reduce_fusion.1
  145.4 1.7 fusion.103
  147.1 3.5 %convolution_convert_fusion.5 = bf16[512,768]{1,0:T(8,128)(2,1)} fusion(bf16[768,3072]{1,0:T(8,128)(2,1)} %get-tuple-element.113, f32[512,768]{1,0:T(8,128)} %get-tuple-element.213, f32[512]{0:T(512)S(1)} %negate_multiply_fusion), kind=kOutput, calls=%fused_computation.120 | convolution fusion | flops 605159424 | bytes 3540992 | tf_op jit(solution)/shard_map/dot_general | solution.py:572
  150.6 2.3 copy.35
  152.8 27.3 %while.29 = (s32[]{:T(128)}, f32[3,4,512,64]{2,3,1,0:T(8,128)S(1)}, f32[3,4,512,64]{2,3,1,0:T(8,128)}, bf16[3,4,512,64]{2,3,1,0:T(8,128)(2,1)}, bf16[3,4,512,64]...) while((s32[]{:T(128)}, f32[3,4,512,64]{2,3,1,0:T(8,128)S(1)}, ...), condition=%wide.region_14.15_spmd.clone, body=%wide.region_12.14_spmd.clone.sunk | while | flops 687339520 | bytes 45415628 | solution.py:743
  153.0 0.8 fusion.162
  154.1 2.5 multiply_reduce_fusion.6
  156.6 1.3 multiply_convert_fusion.4
  158.3 1.6 fusion.164
  159.9 1.2 fusion.165
  161.2 0.9 copy-done.27
  162.0 0.8 fusion.162
  163.2 2.5 multiply_reduce_fusion.6
  165.6 1.3 multiply_convert_fusion.4
  167.4 1.6 fusion.164
  168.9 1.2 fusion.165
  170.2 0.9 copy-done.27
  171.1 0.8 fusion.162
  172.2 2.5 multiply_reduce_fusion.6
  174.7 1.3 multiply_convert_fusion.4
  176.4 1.6 fusion.164
  178.0 1.2 fusion.165
  179.2 0.9 copy-done.27
  180.1 1.9 bitcast_multiply_fusion.2
  182.4 1.2 copy-done.2
  183.6 0.9 fusion.77
  185.3 3.0 add_convert_fusion
  188.3 3.8 %fusion.62.refs_0_ = bf16[768,2304]{1,0:T(8,128)(2,1)} fusion(bf16[512,768]{1,0:T(8,128)(2,1)S(1)} %copy-done.22, bf16[512,768]{0,1:T(8,128)(2,1)S(1)} %bitcast.226, bf16[512,768]{0,1:T(8,128)(2,1)S(1)} %bitcast.209, bf16[512,768]{0,1:T(8,128)(2,1)S(1)} %bitcast.207), kind=kOutput, calls=%fused_computation.76 | convolution fusion | flops 1820786688 | bytes 6684672 | tf_op jit(solution)/shard_map/dot_general | solution.py:578
  192.1 1.9 convolution_convert_fusion.4.refs_1_
  194.1 0.6 copy-done.32
  194.7 4.6 %convolution_convert_fusion.2.refs_2_ = bf16[768,3072]{1,0:T(8,128)(2,1)} fusion(bf16[512,768]{1,0:T(8,128)(2,1)S(1)} %copy-done.6, bf16[512,3072]{1,0:T(8,128)(2,1)S(1)} %copy-done.32), kind=kOutput, calls=%fused_computation.73 | convolution fusion | flops 2418278400 | bytes 8650752 | tf_op jit(solution)/shard_map/dot_general | solution.py:578
  199.3 4.4 %convolution_convert_fusion.1.refs_3_ = bf16[768,3072]{1,0:T(8,128)(2,1)} fusion(bf16[512,768]{1,0:T(8,128)(2,1)S(1)} %copy-done.6, bf16[512,3072]{1,0:T(8,128)(2,1)S(1)} %copy-done.30), kind=kOutput, calls=%fused_computation.72 | convolution fusion | flops 2418278400 | bytes 8650752 | tf_op jit(solution)/shard_map/dot_general | solution.py:578
  203.7 4.5 %convolution_convert_fusion.refs_4_ = bf16[3072,768]{1,0:T(8,128)(2,1)} fusion(bf16[512,3072]{1,0:T(8,128)(2,1)S(1)} %copy-done.34, f32[512,768]{1,0:T(8,128)S(1)} %copy-done.8, f32[512]{0:T(512)S(1)} %negate_multiply_fusion.1), kind=kOutput, calls=%fused_computation.71 | convolution fusion | flops 2419064832 | bytes 9439232 | tf_op jit(solution)/shard_map/dot_general | solution.py:578
  209.2 112.5 %sum_grads.1 = (bf16[96,3072]{1,0:T(8,128)(2,1)}, bf16[96,3072]{1,0:T(8,128)(2,1)}, bf16[96,3072]{1,0:T(8,128)(2,1)}, bf16[96,3072]{1,0:T(8,128)(2,1)}, f32[8,128]{1,0:T(8,128)}) custom-call(bf16[768,2304]{1,0:T(8,128)(2,1)} %fusion.62.refs_0_, bf16[768,768]{1,0:T(8,128)(2,1)} %convolution_convert_fusion.4.refs_1_, ...), custom_call_target="tpu_custom_call" | custom-call | tf_op jit(solution)/shard_map/sum_grads/pallas_call | solution.py:519
  321.7 2.1 slice_convert_fusion.1
  323.8 1.7 slice_convert_fusion.2
  325.5 1.1 convert_element_type.132
  326.6 1.1 convert_element_type.133
  328.3 1.2 copy.37
  (154 shorter events, 9.5 us)
Async XLA Ops:
  0.6 87.3 %copy-start.21 = (bf16[512,768]{1,0:T(8,128)(2,1)S(1)}, bf16[512,768]{1,0:T(8,128)(2,1)}, u32[]{:S(2)}) copy-start(bf16[512,768]{1,0:T(8,128)(2,1)} %param.17) | copy-start | bytes 2359300
  92.4 0.7 copy-start.19
  93.4 1.0 copy-start.10
  93.4 1.0 copy-start.12
  93.4 1.1 copy-start.14
  93.4 1.2 copy-start.23
  105.3 0.9 copy-start.3
  105.3 1.1 copy-start.24
  106.5 2.6 copy-start.18
  109.6 5.3 %slice-start.4 = ((s8[4718592]{0:T(1024)(128)(4,1)}), s8[4194304]{0:T(1024)(128)(4,1)S(1)}, s32[]{:S(2)}) async-start(s8[4718592]{0:T(1024)(128)(4,1)} %bitcast.217), calls=%async_computation.4 | async-start | bytes 8388608
  109.9 5.0 %copy-start.5 = (bf16[512,768]{1,0:T(8,128)(2,1)}, bf16[512,768]{1,0:T(8,128)(2,1)S(1)}, u32[]{:S(2)}) copy-start(bf16[512,768]{1,0:T(8,128)(2,1)S(1)} %fusion.80) | copy-start | bytes 2359300
  110.0 5.0 %slice-start.5 = ((s8[4718592]{0:T(1024)(128)(4,1)}), s8[524288]{0:T(1024)(128)(4,1)S(1)}, s32[]{:S(2)}) async-start(s8[4718592]{0:T(1024)(128)(4,1)} %bitcast.217), calls=%async_computation.5 | async-start | bytes 1048576
  110.0 10.0 %slice-start.8 = ((s8[4718592]{0:T(1024)(128)(4,1)}), s8[4194304]{0:T(1024)(128)(4,1)S(1)}, s32[]{:S(2)}) async-start(s8[4718592]{0:T(1024)(128)(4,1)} %bitcast.221), calls=%async_computation.8 | async-start | bytes 8388608
  114.9 5.0 %copy-start.1 = (f32[512,3072]{1,0:T(8,128)}, f32[512,3072]{1,0:T(8,128)S(1)}, u32[]{:S(2)}) copy-start(f32[512,3072]{1,0:T(8,128)S(1)} %fusion.110) | copy-start | bytes 18874372
  115.0 5.0 %slice-start.9 = ((s8[4718592]{0:T(1024)(128)(4,1)}), s8[524288]{0:T(1024)(128)(4,1)S(1)}, s32[]{:S(2)}) async-start(s8[4718592]{0:T(1024)(128)(4,1)} %bitcast.221), calls=%async_computation.9 | async-start | bytes 1048576
  119.9 2.8 copy-start.33
  122.7 1.1 copy-start
  126.6 12.8 %slice-start = ((s8[4718592]{0:T(1024)(128)(4,1)}), s8[4194304]{0:T(1024)(128)(4,1)S(1)}, s32[]{:S(2)}) async-start(s8[4718592]{0:T(1024)(128)(4,1)} %bitcast.202), calls=%async_computation | async-start | bytes 8388608
  126.6 15.5 %slice-start.6 = ((s8[4718592]{0:T(1024)(128)(4,1)}), s8[4194304]{0:T(1024)(128)(4,1)S(1)}, s32[]{:S(2)}) async-start(s8[4718592]{0:T(1024)(128)(4,1)} %bitcast.219), calls=%async_computation.6 | async-start | bytes 8388608
  130.0 12.1 %copy-start.7 = (f32[512,768]{1,0:T(8,128)}, f32[512,768]{1,0:T(8,128)S(1)}, u32[]{:S(2)}) copy-start(f32[512,768]{1,0:T(8,128)S(1)} %get-tuple-element.215) | copy-start | bytes 4718596
  130.0 9.4 %slice-start.1 = ((s8[4718592]{0:T(1024)(128)(4,1)}), s8[524288]{0:T(1024)(128)(4,1)S(1)}, s32[]{:S(2)}) async-start(s8[4718592]{0:T(1024)(128)(4,1)} %bitcast.202), calls=%async_computation.1 | async-start | bytes 1048576
  130.0 12.2 %slice-start.7 = ((s8[4718592]{0:T(1024)(128)(4,1)}), s8[524288]{0:T(1024)(128)(4,1)S(1)}, s32[]{:S(2)}) async-start(s8[4718592]{0:T(1024)(128)(4,1)} %bitcast.219), calls=%async_computation.7 | async-start | bytes 1048576
  139.4 2.7 copy-start.29
  139.4 2.8 copy-start.31
  152.8 27.3 %copy-start.13 = (f32[512,64]{0,1:T(8,128)S(1)}, f32[512,64]{0,1:T(8,128)}, u32[]{:S(2)}) copy-start(f32[512,64]{0,1:T(8,128)} %copy-done.12) | copy-start | bytes 393220
  153.0 1.1 copy-start.4
  158.3 1.6 copy-start.26
  161.1 0.9 copy-start.27
  162.0 1.1 copy-start.4
  167.4 1.6 copy-start.26
  170.2 0.9 copy-start.27
  171.1 1.1 copy-start.4
  176.4 1.6 copy-start.26
  179.2 0.9 copy-start.27
  180.1 4.4 %slice-start.2 = ((s8[4718592]{0:T(1024)(128)(4,1)}), s8[4194304]{0:T(1024)(128)(4,1)S(1)}, s32[]{:S(2)}) async-start(s8[4718592]{0:T(1024)(128)(4,1)} %bitcast.215), calls=%async_computation.2 | async-start | bytes 8388608
  182.2 1.4 copy-start.2
  182.2 1.4 copy-start.11
  182.2 2.3 slice-start.3
  183.6 1.4 copy-start.9
  183.6 1.6 copy-start.28
  185.3 3.0 copy-start.22
  188.3 3.8 %copy-start.25 = (bf16[3,4,512,64]{2,3,1,0:T(8,128)(2,1)S(1)}, bf16[3,4,512,64]{2,3,1,0:T(8,128)(2,1)}, u32[]{:S(2)}) copy-start(bf16[3,4,512,64]{2,3,1,0:T(8,128)(2,1)} %copy-done.24) | copy-start | bytes 2359300
  192.1 1.9 copy-start.6
  192.1 2.6 copy-start.32
  194.7 4.6 %copy-start.30 = (bf16[512,3072]{1,0:T(8,128)(2,1)S(1)}, bf16[512,3072]{1,0:T(8,128)(2,1)}, u32[]{:S(2)}) copy-start(bf16[512,3072]{1,0:T(8,128)(2,1)} %copy-done.29) | copy-start | bytes 9437188
  199.3 4.4 %copy-start.8 = (f32[512,768]{1,0:T(8,128)S(1)}, f32[512,768]{1,0:T(8,128)}, u32[]{:S(2)}) copy-start(f32[512,768]{1,0:T(8,128)} %copy-done.7) | copy-start | bytes 4718596
  199.3 4.4 %copy-start.34 = (bf16[512,3072]{1,0:T(8,128)(2,1)S(1)}, bf16[512,3072]{1,0:T(8,128)(2,1)}, u32[]{:S(2)}) copy-start(bf16[512,3072]{1,0:T(8,128)(2,1)} %copy-done.33) | copy-start | bytes 9437188
  321.7 3.8 %copy-start.17 = (bf16[96,3072]{1,0:T(8,128)(2,1)S(1)}, bf16[96,3072]{1,0:T(8,128)(2,1)}, u32[]{:S(2)}) copy-start(bf16[96,3072]{1,0:T(8,128)(2,1)} %get-tuple-element.124) | copy-start | bytes 1769476
  321.7 4.9 %copy-start.16 = (bf16[96,3072]{1,0:T(8,128)(2,1)S(1)}, bf16[96,3072]{1,0:T(8,128)(2,1)}, u32[]{:S(2)}) copy-start(bf16[96,3072]{1,0:T(8,128)(2,1)} %get-tuple-element.125) | copy-start | bytes 1769476
  323.8 3.9 %copy-start.15 = (bf16[96,3072]{1,0:T(8,128)(2,1)S(1)}, bf16[96,3072]{1,0:T(8,128)(2,1)}, u32[]{:S(2)}) copy-start(bf16[96,3072]{1,0:T(8,128)(2,1)} %get-tuple-element.126) | copy-start | bytes 1769476
  327.7 1.8 copy-start.20
